TPU v7x, 32 devices: a whole 2x2x4 slice. The times are simulated.
32 devices in a mesh: section: 4 (over y, x), seq: 2 (over core), exp: 4 (over z).
Axes of the slice: x: 2, y: 2, z: 4, core: 2. Of those that a mesh axis runs over, the one named last changes fastest.
Arguments:
- latent: bfloat16 [8, 8, 64, 384], P('section', 'seq', 'exp'), may hold values from -6 to 6
- cotangent: bfloat16 [8, 8, 64, 384], P('section', 'seq', 'exp'), may hold values from -6 to 6
- gain_one: float32 [384], replicated, may hold values from 0.5 to 2
- gain_two: float32 [384], replicated, may hold values from 0.5 to 2
- kernel_one: bfloat16 [3, 3, 3, 384, 384], P(None, None, None, 'exp'), may hold values from -0.0625 to 0.0625
- kernel_two: bfloat16 [3, 3, 3, 384, 384], P(None, None, None, 'exp'), may hold values from -0.0625 to 0.0625
Outputs:
- block_out: bfloat16 [8, 8, 64, 384], P('section', 'seq', 'exp')
- latent_grad: bfloat16 [8, 8, 64, 384], P('section', 'seq', 'exp')
All inputs are finite; a program needn't handle non-finite values.
Results may differ from a plain program's by a relative error of at most 0.015.
Values may be sent and summed in bfloat16 or wider, within the bound.
A program may use at most 64 MiB of HBM per device.

v0:
```python
import functools

import jax
import jax.numpy as jnp
from jax import lax
from jax.experimental import pallas as pl
from jax.experimental.pallas import tpu as pltpu
from jax.sharding import PartitionSpec as P

epsilon = 1e-06
MESH = pl.DeviceIdType.MESH
bf16, f32 = jnp.bfloat16, jnp.float32


def normalize(values, gain):
    inverse = lax.rsqrt(jnp.mean(values * values, axis=-1, keepdims=True) + epsilon)
    return values * inverse * gain, inverse


def norm_backward(values, inverse, gain, upstream):
    scaled = upstream * gain
    mean = jnp.mean(values * scaled, axis=-1, keepdims=True)
    return inverse * scaled - values * (inverse * inverse * inverse) * mean


def silu(normed):
    return normed / (1.0 + jnp.exp(-normed))


def silu_slope(normed):
    sigma = 1.0 / (1.0 + jnp.exp(-normed))
    return sigma * (1.0 + normed * (1.0 - sigma))


def shift_sum(taps, width, size):
    rows = taps.shape[0]
    column = lax.rem(lax.broadcasted_iota(jnp.int32, (rows, size), 0), width)
    low = pltpu.roll(taps[:, :size], 1, axis=0)
    high = pltpu.roll(taps[:, 2 * size :], rows - 1, axis=0)
    return (
        taps[:, size : 2 * size]
        + jnp.where(column == 0, 0.0, low)
        + jnp.where(column == width - 1, 0.0, high)
    )


def stage(index, sizes, act, grad, w_fwd, w_bwd, bufs, send, recv, w_ready):
    S, Q, Z = sizes
    xp, qs, qp, yf, rf, rp, yb, rb = bufs
    F, R, W, C = act.shape
    O = w_fwd.shape[3]
    WW = W * Z
    OP = -(-O // 128) * 128
    s, q, z = lax.axis_index("section"), lax.axis_index("seq"), lax.axis_index("exp")
    has_next, has_prev = s < S - 1, s > 0
    has_high, has_low = q < Q - 1, q > 0
    nxt, prv = jnp.minimum(s + 1, S - 1), jnp.maximum(s - 1, 0)
    upper, lower = jnp.minimum(q + 1, Q - 1), jnp.maximum(q - 1, 0)
    mine = pl.ds(pl.multiple_of(z * W, W), W)
    body = pl.ds(1, R)

    def peer(d):
        return lax.rem(z + d, Z)

    def columns(d):
        return pl.ds(pl.multiple_of(peer(d) * W, W), W)

    def remote(src, dst, slot, device):
        return pltpu.make_async_remote_copy(
            src_ref=src,
            dst_ref=dst,
            send_sem=send.at[index, slot],
            recv_sem=recv.at[index, slot],
            device_id=device,
            device_id_type=MESH,
        )

    def q_own(d):
        return remote(qs.at[peer(d)], qp.at[pl.ds(0, F), body, mine], d, (s, q, peer(d)))

    def q_prev(d):
        return remote(
            qs.at[peer(d), pl.ds(0, 2)], qp.at[pl.ds(F, 2), body, mine], Z + d, (prv, q, peer(d))
        )

    def block_at(owner):
        return xp.at[:, body, pl.ds(pl.multiple_of(jnp.clip(owner, 0, Z - 1) * W, W), W)]

    def x_right(k):
        held = block_at(z - (k - 1))
        return remote(act if k == 1 else held, held, 2 * Z + k, (s, q, jnp.minimum(z + 1, Z - 1)))

    def x_left(k):
        held = block_at(z + (k - 1))
        return remote(act if k == 1 else held, held, 6 * Z + 4 + k, (s, q, jnp.maximum(z - 1, 0)))

    def sends_right(k):
        return jnp.logical_and(z >= k - 1, z < Z - 1)

    def sends_left(k):
        return jnp.logical_and(z <= Z - k, z > 0)

    def pass_on(k):
        @pl.when(sends_right(k))
        def _():
            x_right(k).start()

        @pl.when(sends_left(k))
        def _():
            x_left(k).start()

    def arrive(k):
        @pl.when(z >= k)
        def _():
            x_right(k).wait_recv()

        @pl.when(z <= Z - 1 - k)
        def _():
            x_left(k).wait_recv()

        if k < Z - 1:
            pass_on(k + 1)

    def b_own(d):
        return remote(yb.at[:, :, columns(d)], rb.at[d], 3 * Z + d, (s, q, peer(d)))

    def f_own(d):
        return remote(
            yf.at[pl.ds(0, F), :, columns(d)], rf.at[z], 4 * Z + d, (s, q, peer(d))
        )

    def f_next(d):
        return remote(
            yf.at[pl.ds(F, 2), :, columns(d)], rp.at[z], 5 * Z + d, (nxt, q, peer(d))
        )

    def to_high(buf, slot):
        return remote(buf.at[:, R], buf.at[:, 0], slot, (s, upper, z))

    def to_low(buf, slot):
        return remote(buf.at[:, 1], buf.at[:, R + 1], slot, (s, lower, z))

    def exchange_rows(buf, slot):
        @pl.when(has_high)
        def _():
            to_high(buf, slot).start()

        @pl.when(has_low)
        def _():
            to_low(buf, slot + 1).start()

        @pl.when(jnp.logical_not(has_low))
        def _():
            buf[:, 0] = jnp.zeros_like(buf[:, 0])

        @pl.when(jnp.logical_not(has_high))
        def _():
            buf[:, R + 1] = jnp.zeros_like(buf[:, R + 1])

        @pl.when(has_low)
        def _():
            to_high(buf, slot).wait_recv()

        @pl.when(has_high)
        def _():
            to_low(buf, slot + 1).wait_recv()

    for m in range(Z):
        qs[m] = grad[:, :, :, m * O : (m + 1) * O]
    for d in range(1, Z):
        q_own(d).start()

    @pl.when(has_prev)
    def _():
        for d in range(Z):
            q_prev(d).start()

    if Z > 1:
        pass_on(1)
    qp[pl.ds(0, F), body, mine] = qs[z]
    xp[:, body, mine] = act[...]

    @pl.when(jnp.logical_not(has_next))
    def _():
        qp[pl.ds(F, 2), body] = jnp.zeros((2, R, WW, O), bf16)

    for d in range(1, Z):
        q_own(d).wait_recv()

    @pl.when(has_next)
    def _():
        for d in range(Z):
            q_prev(d).wait_recv()

    exchange_rows(qp, 6 * Z)
    arrived = 1
    w_ready[1].wait()

    def padded(value, axis):
        shape = list(value.shape)
        shape[axis] = OP - O
        if OP == O:
            return value
        return jnp.concatenate([value, jnp.zeros(shape, value.dtype)], axis=axis)

    for f in range(F):
        if arrived < Z:
            arrive(arrived)
            arrived += 1
        total = None
        for i in range(3):
            lhs = jnp.concatenate(
                [padded(qp[f + i, pl.ds(j, R)].reshape(R * WW, O), 1) for j in range(3)], axis=1
            )
            rhs = jnp.concatenate(
                [
                    jnp.concatenate(
                        [padded(w_bwd[2 - i, 2 - j, 2 - l], 0) for l in range(3)], axis=1
                    )
                    for j in range(3)
                ],
                axis=0,
            )
            part = jnp.dot(lhs, rhs, preferred_element_type=f32)
            total = part if total is None else total + part
        yb[f] = shift_sum(total, WW, C).astype(bf16).reshape(R, WW, C)
    for d in range(1, Z):
        b_own(d).start()

    for k in range(arrived, Z):
        arrive(k)
    exchange_rows(xp, 6 * Z + 2)
    w_ready[0].wait()
    for t in list(range(F, F + 2)) + list(range(F)):
        total = None
        for i in range(3):
            f = t + i - 2
            if not 0 <= f < F:
                continue
            lhs = jnp.concatenate(
                [xp[f, pl.ds(j, R)].reshape(R * WW, C) for j in range(3)], axis=1
            )
            rhs = jnp.concatenate(
                [
                    jnp.concatenate([padded(w_fwd[i, j, l], 0) for l in range(3)], axis=0)
                    for j in range(3)
                ],
                axis=1,
            )
            part = lax.dot_general(
                lhs, rhs, (((1,), (1,)), ((), ())), preferred_element_type=f32
            )
            total = part if total is None else total + part
        yf[t] = shift_sum(total, WW, OP)[:, :O].astype(bf16).reshape(R, WW, O)
        if t == F + 1:

            @pl.when(has_next)
            def _():
                for d in range(Z):
                    f_next(d).start()

    for d in range(1, Z):
        f_own(d).start()
    rf[z] = yf[pl.ds(0, F), :, mine]

    @pl.when(jnp.logical_not(has_prev))
    def _():
        rp[...] = jnp.zeros_like(rp)

    for d in range(1, Z):
        b_own(d).wait_recv()
    result_b = yb[:, :, mine].astype(f32)
    for d in range(1, Z):
        result_b = result_b + rb[d].astype(f32)
    result_b = result_b.reshape(F * R * W, C)

    for d in range(1, Z):
        f_own(d).wait_recv()

    @pl.when(has_prev)
    def _():
        for d in range(Z):
            f_next(d).wait_recv()

    chunks = []
    for m in range(Z):
        head = rf[m, pl.ds(0, 2)].astype(f32) + rp[m].astype(f32)
        if F > 2:
            head = jnp.concatenate([head, rf[m, pl.ds(2, F - 2)].astype(f32)], axis=0)
        chunks.append(head.reshape(F * R * W, O))
    result_f = jnp.concatenate(chunks, axis=1)

    def drain():
        for k in range(1, Z):

            @pl.when(sends_right(k))
            def _():
                x_right(k).wait_send()

            @pl.when(sends_left(k))
            def _():
                x_left(k).wait_send()

        for d in range(1, Z):
            q_own(d).wait_send()
            b_own(d).wait_send()
            f_own(d).wait_send()

        @pl.when(has_prev)
        def _():
            for d in range(Z):
                q_prev(d).wait_send()

        @pl.when(has_next)
        def _():
            for d in range(Z):
                f_next(d).wait_send()

        for buf, slot in ((qp, 6 * Z), (xp, 6 * Z + 2)):

            @pl.when(has_high)
            def _():
                to_high(buf, slot).wait_send()

            @pl.when(has_low)
            def _():
                to_low(buf, slot + 1).wait_send()

    return result_f, result_b, drain


def kernel(sizes, latent, cotangent, gain_one, gain_two, kernel_one, kernel_two, out, latent_grad, *scratch):
    S, Q, Z = sizes
    act_one, act_two, grad_two_ref, w_one, w_two, send, recv, w_sem = scratch[:8]
    bufs_one, bufs_two = scratch[8:16], scratch[16:24]
    F, R, W, C = latent.shape
    rows = F * R * W
    s, q, z = lax.axis_index("section"), lax.axis_index("seq"), lax.axis_index("exp")

    load_one = pltpu.make_async_copy(kernel_one, w_one, w_sem.at[0])
    load_two = pltpu.make_async_copy(kernel_two, w_two, w_sem.at[1])
    load_two.start()
    load_one.start()

    barrier = pltpu.get_barrier_semaphore()

    def greet(device):
        pl.semaphore_signal(barrier, inc=1, device_id=device, device_id_type=MESH)

    for d in range(1, Z):
        greet((s, q, lax.rem(z + d, Z)))
    for condition, step in ((s < S - 1, 1), (s > 0, -1)):

        @pl.when(condition)
        def _():
            for d in range(Z):
                greet((s + step, q, lax.rem(z + d, Z)))

    for condition, step in ((q < Q - 1, 1), (q > 0, -1)):

        @pl.when(condition)
        def _():
            greet((s, q + step, z))

    source = latent[...].reshape(rows, C).astype(f32)
    g_one, g_two = gain_one[...].reshape(1, C), gain_two[...].reshape(1, C)
    normed_one, inverse_one = normalize(source, g_one)
    act_one[...] = silu(normed_one).astype(bf16).reshape(F, R, W, C)

    sections = (s < S - 1).astype(jnp.int32) + (s > 0).astype(jnp.int32)
    neighbours = (q < Q - 1).astype(jnp.int32) + (q > 0).astype(jnp.int32)
    pl.semaphore_wait(barrier, Z - 1 + Z * sections + neighbours)

    class Done:
        def wait(self):
            pass

    inner, grad_two, drain_one = stage(
        0, sizes, act_one, cotangent, w_one, w_two, bufs_one, send, recv, (load_one, load_two)
    )
    normed_two, inverse_two = normalize(inner, g_two)
    act_two[...] = silu(normed_two).astype(bf16).reshape(F, R, W, C)
    grad_inner = norm_backward(inner, inverse_two, g_two, grad_two * silu_slope(normed_two))
    grad_two_ref[...] = grad_inner.astype(bf16).reshape(F, R, W, C)

    branch, grad_one, drain_two = stage(
        1, sizes, act_two, grad_two_ref, w_two, w_one, bufs_two, send, recv, (Done(), Done())
    )
    source = latent[...].reshape(rows, C).astype(f32)
    out[...] = (source + branch).astype(bf16).reshape(F, R, W, C)
    normed_one, inverse_one = normalize(source, g_one)
    grad = norm_backward(source, inverse_one, g_one, grad_one * silu_slope(normed_one))
    upstream = cotangent[...].reshape(rows, C).astype(f32)
    latent_grad[...] = (upstream + grad).astype(bf16).reshape(F, R, W, C)
    drain_one()
    drain_two()


def local(sizes, latent, cotangent, gain_one, gain_two, kernel_one, kernel_two):
    S, Q, Z = sizes
    F, R, W, C = latent.shape
    O = kernel_one.shape[3]
    WW = W * Z
    block = pltpu.VMEM((F, R, W, C), bf16)
    weight = pltpu.VMEM(kernel_one.shape, bf16)
    bufs = [
        pltpu.VMEM((F, R + 2, WW, C), bf16),
        pltpu.VMEM((Z, F, R, W, O), bf16),
        pltpu.VMEM((F + 2, R + 2, WW, O), bf16),
        pltpu.VMEM((F + 2, R, WW, O), bf16),
        pltpu.VMEM((Z, F, R, W, O), bf16),
        pltpu.VMEM((Z, 2, R, W, O), bf16),
        pltpu.VMEM((F, R, WW, C), bf16),
        pltpu.VMEM((Z, F, R, W, C), bf16),
    ]
    slots = 7 * Z + 4
    vmem = pl.BlockSpec(memory_space=pltpu.VMEM)
    hbm = pl.BlockSpec(memory_space=pl.ANY)
    return pl.pallas_call(
        functools.partial(kernel, sizes),
        out_shape=[jax.ShapeDtypeStruct((F, R, W, C), bf16)] * 2,
        in_specs=[vmem, vmem, vmem, vmem, hbm, hbm],
        out_specs=[vmem, vmem],
        scratch_shapes=[
            block,
            block,
            block,
            weight,
            weight,
            pltpu.SemaphoreType.DMA((2, slots)),
            pltpu.SemaphoreType.DMA((2, slots)),
            pltpu.SemaphoreType.DMA((2,)),
            *bufs,
            *bufs,
        ],
        compiler_params=pltpu.CompilerParams(
            collective_id=0, has_side_effects=True, vmem_limit_bytes=60 * 1024 * 1024
        ),
    )(latent, cotangent, gain_one, gain_two, kernel_one, kernel_two)


def solution(mesh):
    sizes = (mesh.shape["section"], mesh.shape["seq"], mesh.shape["exp"])
    spread = P("section", "seq", "exp", None)
    split = P(None, None, None, "exp", None)
    return jax.shard_map(
        functools.partial(local, sizes),
        mesh=mesh,
        in_specs=(spread, spread, P(), P(), split, split),
        out_specs=(spread, spread),
        check_vma=False,
    )
```

profile of v0, /device:TPU:0, one launch (start us, length us, event | category | flops | bytes accessed | tf_op | source)
XLA Modules:
  0.0 72.8 jit_solution(6876027047869605908)
XLA Ops:
  0.6 69.1 %shard_map.77 = (bf16[2,4,16,384]{3,2,1,0:T(8,128)(2,1)}, bf16[2,4,16,384]{3,2,1,0:T(8,128)(2,1)}) custom-call(bf16[2,4,16,384]{3,2,1,0:T(8,128)(2,1)} %latent.1, bf16[2,4,16,384]{3,2,1,0:T(8,128)(2,1)} %cotangent.1, f32[384]{0:T(512)} %gain_one.1, f32[384]{0:T(512)} %gain_two.1, bf16[3,3,3,96,384]{4,3,2,1,0:T(8,128)(2,1)} %kernel_one.1, ...), custom_call_target="tpu_custom_call" | custom-call | tf_op jit(solution)/shard_map/pallas_call | solution.py:419
  69.7 1.5 %copy.10 = bf16[2,4,16,384]{3,2,1,0:T(8,128)(2,1)} copy(bf16[2,4,16,384]{3,2,1,0:T(8,128)(2,1)} %get-tuple-element.4) | data formatting | bytes 196608
  71.3 1.5 %copy.11 = bf16[2,4,16,384]{3,2,1,0:T(8,128)(2,1)} copy(bf16[2,4,16,384]{3,2,1,0:T(8,128)(2,1)} %get-tuple-element.5) | data formatting | bytes 196608
where the time goes:
time: 73 us; the launch traced here: 72.8 us
  Pallas kernels  69.1 us (95%)
  local copies, waits for them, and re-layouts  3.09 us (4%)
    pallas_call x1, Pallas kernels, local(): pl.pallas_call(functools.partial(kernel, sizes), out_shape=[jax.ShapeDtyp...  69.1 us
    unnamed x2, local copies, waits for them, and re-layouts  3.09 us

commit v1 on v0

v1 whole, which is shorter than its diff:
```python
import functools

import jax
import jax.numpy as jnp
from jax import lax
from jax.experimental import pallas as pl
from jax.experimental.pallas import tpu as pltpu
from jax.sharding import PartitionSpec as P

epsilon = 1e-06
MESH = pl.DeviceIdType.MESH
bf16, f32 = jnp.bfloat16, jnp.float32
EXACT = lax.Precision.HIGHEST


def normalize(values, gain):
    inverse = lax.rsqrt(jnp.mean(values * values, axis=-1, keepdims=True) + epsilon)
    return values * inverse * gain, inverse


def norm_backward(values, inverse, gain, upstream):
    scaled = upstream * gain
    mean = jnp.mean(values * scaled, axis=-1, keepdims=True)
    return inverse * scaled - values * (inverse * inverse * inverse) * mean


def silu(normed):
    return normed / (1.0 + jnp.exp(-normed))


def silu_slope(normed):
    sigma = 1.0 / (1.0 + jnp.exp(-normed))
    return sigma * (1.0 + normed * (1.0 - sigma))


def shift_sum(taps, width, size):
    rows = taps.shape[0]
    column = lax.rem(lax.broadcasted_iota(jnp.int32, (rows, size), 0), width)
    low = pltpu.roll(taps[:, :size], 1, axis=0)
    high = pltpu.roll(taps[:, 2 * size :], rows - 1, axis=0)
    return (
        taps[:, size : 2 * size]
        + jnp.where(column == 0, 0.0, low)
        + jnp.where(column == width - 1, 0.0, high)
    )


def pad_to(value, axis, size):
    shape = list(value.shape)
    if shape[axis] == size:
        return value
    shape[axis] = size - shape[axis]
    return jnp.concatenate([value, jnp.zeros(shape, value.dtype)], axis=axis)


class Links:
    def __init__(self, send, recv):
        self.send, self.recv, self.all = send, recv, []

    def copy(self, src, dst, device, sends=True, receives=True):
        made = Copy(self, len(self.all), src, dst, device, sends, receives)
        self.all.append(made)
        return made

    def drain(self):
        for made in self.all:
            made.drain()


class Copy:
    def __init__(self, links, slot, src, dst, device, sends, receives):
        self.made = lambda: pltpu.make_async_remote_copy(
            src_ref=src,
            dst_ref=dst,
            send_sem=links.send.at[slot],
            recv_sem=links.recv.at[slot],
            device_id=device,
            device_id_type=MESH,
        )
        self.sends, self.receives = sends, receives

    def start(self):
        when(self.sends, lambda: self.made().start())

    def wait(self):
        when(self.receives, lambda: self.made().wait_recv())

    def drain(self):
        when(self.sends, lambda: self.made().wait_send())


def when(condition, action):
    if condition is True:
        action()
    else:
        pl.when(condition)(action)


def kernel(sizes, latent, cotangent, gain_one, gain_two, kernel_one, kernel_two, out, latent_grad, *scratch):
    S, Q, Z = sizes
    (
        w_one, w_two, w_gap, act, xp, qs, qp, gs, gr, fs, fr, vall, st, gains,
        xq, gi, gh, gu, gd, qq, yf, rf, rp, yb, rb, g_sum, send, recv, w_sem,
    ) = scratch
    F, R, W, C = latent.shape
    O = kernel_one.shape[3]
    WW = W * Z
    OP = -(-O // 128) * 128
    rows = F * R * W
    s, q, z = lax.axis_index("section"), lax.axis_index("seq"), lax.axis_index("exp")
    has_next, has_prev = s < S - 1, s > 0
    has_high, has_low = q < Q - 1, q > 0
    both = jnp.logical_and
    nxt, prv = jnp.minimum(s + 1, S - 1), jnp.maximum(s - 1, 0)
    upper, lower = jnp.minimum(q + 1, Q - 1), jnp.maximum(q - 1, 0)
    body, own, halo = pl.ds(1, R), pl.ds(0, F), pl.ds(F, 2)
    two = pl.ds(0, 2)
    links = Links(send, recv)

    load_one = pltpu.make_async_copy(kernel_one, w_one, w_sem.at[0])
    load_two = pltpu.make_async_copy(kernel_two, w_two, w_sem.at[1])
    load_two.start()
    load_one.start()

    barrier = pltpu.get_barrier_semaphore()

    def greet(device):
        pl.semaphore_signal(barrier, inc=1, device_id=device, device_id_type=MESH)

    for d in range(1, Z):
        greet((s, q, lax.rem(z + d, Z)))
    for near, step in ((has_next, 1), (has_prev, -1)):

        @pl.when(near)
        def _():
            for d in range(Z):
                greet((s + step, q, lax.rem(z + d, Z)))

        for side, move in ((has_high, 1), (has_low, -1)):

            @pl.when(both(near, side))
            def _():
                greet((s + step, q + move, z))

    for side, move in ((has_high, 1), (has_low, -1)):

        @pl.when(side)
        def _():
            greet((s, q + move, z))

    def peer(d):
        return lax.rem(z + d + Z, Z)

    def block(index):
        return pl.ds(pl.multiple_of(index * W, W), W)

    def gather(source, at):
        arrive = []
        for d in range(1, Z):
            for sign in (1, -1):
                if d <= 2:
                    target, sends = z + sign * d, (z + d < Z) if sign > 0 else (z >= d)
                    src, dst = source, at(z)
                else:
                    target = z + sign
                    held = z - sign * (d - 1)
                    sends = both(z < Z - 1, z >= d - 1) if sign > 0 else both(z > 0, z <= Z - d)
                    src = dst = at(jnp.clip(held, 0, Z - 1))
                receives = (z >= d) if sign > 0 else (z + d < Z)
                target = jnp.clip(target, 0, Z - 1)
                arrive.append((d, z - sign * d, links.copy(src, dst, (s, q, target), sends, receives)))
        return arrive

    def gather_start(arrive):
        for d in (2, 1):
            for distance, _, made in arrive:
                if distance == d:
                    made.start()

    def gather_wait(arrive, d, use=None):
        for distance, owner, made in arrive:
            if distance == d:
                made.wait()
        for distance, owner, made in arrive:
            if distance == d + 1 and d >= 2:
                made.start()
        if use is not None:
            for distance, owner, made in arrive:
                if distance == d:
                    when(made.receives, functools.partial(use, owner))

    q_own = {d: links.copy(qs.at[peer(d)], qp.at[own, body, block(z)], (s, q, peer(d))) for d in range(1, Z)}
    q_next = {
        d: links.copy(
            qp.at[two, body, block(peer(-d))], qp.at[halo, body, block(peer(-d))], (prv, q, z), has_prev, has_next
        )
        for d in range(Z)
    }

    def rows_out(src, dst, device, towards):
        sides = (has_high, has_low) if towards > 0 else (has_low, has_high)
        return links.copy(src, dst, device, *sides)

    q_rows = [
        rows_out(qp.at[own, R], qp.at[own, 0], (s, upper, z), 1),
        rows_out(qp.at[own, 1], qp.at[own, R + 1], (s, lower, z), -1),
    ]
    q_corner = [
        links.copy(qp.at[two, R], qp.at[halo, 0], (prv, upper, z), both(has_prev, has_high), both(has_next, has_low)),
        links.copy(qp.at[two, 1], qp.at[halo, R + 1], (prv, lower, z), both(has_prev, has_low), both(has_next, has_high)),
    ]
    x_rows = [
        rows_out(xp.at[:, R], xp.at[:, 0], (s, upper, z), 1),
        rows_out(xp.at[:, 1], xp.at[:, R + 1], (s, lower, z), -1),
    ]
    x_all = gather(act, lambda owner: xp.at[:, body, block(owner)])
    g_out = {
        (d, f): links.copy(gs.at[peer(d), f], gr.at[d, f], (s, q, peer(d))) for d in range(1, Z) for f in range(F)
    }
    f_out = [links.copy(fs.at[t], fr.at[t], (nxt, q, z), has_next, has_prev) for t in range(2)]
    v_all = gather(vall.at[z], lambda owner: vall.at[owner])
    sums = [{d: links.copy(st.at[k, 0], st.at[k, d], (s, q, peer(d))) for d in range(1, Z)} for k in range(2)]
    xq_rows = [
        rows_out(xq.at[:, :, R], xq.at[:, :, 0], (s, upper, z), 1),
        rows_out(xq.at[:, :, 1], xq.at[:, :, R + 1], (s, lower, z), -1),
    ]
    gi_next = links.copy(gi.at[two], gh, (prv, q, z), has_prev, has_next)
    gi_rows = [
        rows_out(gi.at[:, R - 1], gd.at[own], (s, upper, z), 1),
        rows_out(gi.at[:, 0], gu.at[own], (s, lower, z), -1),
    ]
    gi_corner = [
        links.copy(gi.at[two, R - 1], gd.at[halo], (prv, upper, z), both(has_prev, has_high), both(has_next, has_low)),
        links.copy(gi.at[two, 0], gu.at[halo], (prv, lower, z), both(has_prev, has_low), both(has_next, has_high)),
    ]
    b_out = {
        (d, f): links.copy(yb.at[f, :, block(peer(d))], rb.at[d, f], (s, q, peer(d)))
        for d in range(1, Z)
        for f in range(F)
    }
    y_own = {d: links.copy(yf.at[own, :, block(peer(d))], rf.at[z], (s, q, peer(d))) for d in range(1, Z)}
    y_next = {
        d: links.copy(yf.at[halo, :, block(peer(d))], rp.at[z], (nxt, q, peer(d)), has_next, has_prev)
        for d in range(Z)
    }

    lane = lax.broadcasted_iota(jnp.int32, (8, C), 1)
    group = lax.broadcasted_iota(jnp.int32, (8, C), 0)
    segments = jnp.where(both(lane >= group * O, lane < group * O + O), 1.0, 0.0).astype(f32)

    def pack(value, offset=0):
        count = value.shape[0] // WW
        grouped = value.reshape(count, Z, W, value.shape[1])
        return jnp.concatenate(
            [grouped[:, m].reshape(count * W, value.shape[1])[:, offset : offset + O] for m in range(Z)], axis=1
        )

    def unpack(packed, m):
        return pad_to(packed[:, m * O : (m + 1) * O], 1, OP)

    def segment_sums(value):
        return lax.dot_general(segments, value, (((1,), (1,)), ((), ())), precision=EXACT, preferred_element_type=f32)

    def spread(tile):
        return lax.dot_general(tile, segments, (((0,), (0,)), ((), ())), precision=EXACT, preferred_element_type=f32)

    def rhs_forward(w, i, K):
        return jnp.concatenate(
            [jnp.concatenate([pad_to(w[i, j, l], 0, OP) for l in range(3)], axis=0) for j in range(3)], axis=1
        )

    def rhs_backward(w, i):
        return jnp.concatenate(
            [jnp.concatenate([pad_to(w[2 - i, 2 - j, 2 - l], 0, OP) for l in range(3)], axis=1) for j in range(3)],
            axis=0,
        )

    def forward(lhs_of, w, t):
        total = None
        for i in range(3):
            f = t + i - 2
            if not 0 <= f < F:
                continue
            part = lax.dot_general(
                lhs_of(f), rhs_forward(w, i, None), (((1,), (1,)), ((), ())), preferred_element_type=f32
            )
            total = part if total is None else total + part
        return shift_sum(total, WW, OP)[:, :O]

    def backward(qbuf, w, f, taps):
        total = None
        for i in taps:
            lhs = jnp.concatenate(
                [pad_to(qbuf[f + i, pl.ds(j, R)].reshape(R * WW, qbuf.shape[3]), 1, OP) for j in range(3)], axis=1
            )
            part = jnp.dot(lhs, rhs_backward(w, i), preferred_element_type=f32)
            total = part if total is None else total + part
        return total

    source = latent[...].reshape(rows, C).astype(f32)
    g_one, g_two = gain_one[...].reshape(1, C), gain_two[...].reshape(1, C)
    normed_one, _ = normalize(source, g_one)
    act[...] = silu(normed_one).astype(bf16).reshape(F, R, W, C)
    for m in range(Z):
        qs[m] = cotangent[:, :, :, m * O : (m + 1) * O]

    near = has_next.astype(jnp.int32) + has_prev.astype(jnp.int32)
    sides = has_high.astype(jnp.int32) + has_low.astype(jnp.int32)
    pl.semaphore_wait(barrier, Z - 1 + Z * near + sides + near * sides)

    for d in sorted(range(1, Z), key=lambda d: -abs(2 * d - Z)):
        q_own[d].start()
    gather_start(x_all)
    qp[own, body, block(z)] = qs[z]
    xp[:, body, block(z)] = act[...]
    q_next[0].start()

    def zero(ref, index):
        ref[index] = jnp.zeros_like(ref[index])

    full = slice(None)

    @pl.when(jnp.logical_not(has_next))
    def _():
        zero(qp, (halo,))
        zero(qq, (halo,))

    for missing, row in ((jnp.logical_not(has_low), 0), (jnp.logical_not(has_high), R + 1)):

        @pl.when(missing)
        def _():
            zero(qp, (full, row))
            zero(qq, (full, row))
            zero(xp, (full, row))
            zero(xq, (full, full, row))

    @pl.when(jnp.logical_not(has_prev))
    def _():
        zero(fr, (full,))
        zero(rp, (full,))

    for m in range(Z):
        gains[m] = jnp.broadcast_to(jnp.concatenate([g_two[:, m * O : (m + 1) * O]] * Z, axis=1), (8, C))

    for d in range(1, Z):
        q_own[d].wait()
        q_next[d].start()
    for made in q_rows + q_corner:
        made.start()
    gather_wait(x_all, 2)
    load_two.wait()
    for i in range(3):
        for j in range(3):
            for l in range(3):
                w = w_two[i, j, l].astype(f32)
                w_gap[i, j, l] = jnp.concatenate(
                    [pad_to(w[:, m * O : (m + 1) * O], 1, OP) for m in range(Z)], axis=1
                ).astype(bf16)
    for made in q_rows:
        made.wait()
    for d in range(Z):
        q_next[d].wait()
    for made in q_corner:
        made.wait()
    for f in range(F):
        total = shift_sum(backward(qp, w_two, f, range(3)), WW, C)
        for m in range(Z):
            gs[m, f] = pack(total, m * O).astype(bf16).reshape(R, W, C)
        for d in sorted(range(1, Z), key=lambda d: -abs(2 * d - Z)):
            g_out[d, f].start()

    gather_wait(x_all, 1)
    for d in range(3, Z):
        gather_wait(x_all, d)
    for made in x_rows:
        made.start()
    load_one.wait()
    for made in x_rows:
        made.wait()

    def lhs_one(f):
        return jnp.concatenate([xp[f, pl.ds(j, R)].reshape(R * WW, C) for j in range(3)], axis=1)

    for t in (F + 1, F):
        fs[t - F] = pack(forward(lhs_one, w_one, t)).astype(bf16).reshape(R, W, C)
        f_out[t - F].start()
    inner = [pack(forward(lhs_one, w_one, t)) for t in range(F)]
    for made in f_out:
        made.wait()
    for t in range(2):
        inner[t] = inner[t] + fr[t].reshape(R * W, C).astype(f32)
    inner = jnp.concatenate(inner, axis=0)
    vall[z] = inner.astype(bf16).reshape(F, R, W, C)
    st[0, 0] = segment_sums(inner * inner)
    for d in range(1, Z):
        sums[0][d].start()
    gather_start(v_all)

    grad_two = gs[z].astype(f32)
    for d in range(1, Z):
        for f in range(F):
            g_out[d, f].wait()
        grad_two = grad_two + gr[d].astype(f32)
    grad_two = grad_two.reshape(rows, C)
    squares = st[0, 0]
    for d in range(1, Z):
        sums[0][d].wait()
        squares = squares + st[0, d]
    inverse = lax.rsqrt(squares / C + epsilon)
    inverse_wide = spread(inverse)
    gain = gains[z][0:1]
    scaled = grad_two * silu_slope(inner * inverse_wide * gain) * gain
    st[1, 0] = segment_sums(inner * scaled)
    for d in range(1, Z):
        sums[1][d].start()

    def activate(owner):
        value = vall[owner].reshape(rows, C).astype(f32)
        active = silu(value * spread(inverse) * gains[owner][0:1])
        for m in range(Z):
            xq[owner, :, body, m * W : (m + 1) * W] = unpack(active, m).astype(bf16).reshape(F, R, W, OP)

    activate(z)
    gather_wait(v_all, 2, activate)
    gather_wait(v_all, 1, activate)

    means = st[1, 0]
    for d in range(1, Z):
        sums[1][d].wait()
        means = means + st[1, d]
    factor = spread(inverse * inverse * inverse * means / C)
    grad_inner = (inverse_wide * scaled - inner * factor).astype(bf16)
    gi[...] = grad_inner.reshape(F, R, W, C)
    gi_next.start()
    for made in gi_rows + gi_corner:
        made.start()

    def place(ref, frames, band, count):
        value = ref.reshape(count, C).astype(f32)
        for m in range(Z):
            piece = unpack(value, m).astype(bf16)
            qq[frames, band, m * W : (m + 1) * W] = piece.reshape(
                qq.at[frames, band, m * W : (m + 1) * W].shape
            )

    for d in range(3, Z):
        gather_wait(v_all, d, activate)
    for made in xq_rows:
        made.start()
    place(gi[...], own, body, rows)
    for made in xq_rows:
        made.wait()

    def lhs_two(f):
        return jnp.concatenate(
            [xq[m, f, pl.ds(j, R)].reshape(R * WW, OP) for j in range(3) for m in range(Z)], axis=1
        )

    for t in (F, F + 1):
        yf[t] = forward(lhs_two, w_gap, t).astype(bf16).reshape(R, WW, O)
    for d in range(Z):
        y_next[d].start()
    for t in range(F):
        yf[t] = forward(lhs_two, w_gap, t).astype(bf16).reshape(R, WW, O)
    for d in range(1, Z):
        y_own[d].start()
    rf[z] = yf[own, :, block(z)]

    for made in gi_rows + gi_corner + [gi_next]:
        made.wait()

    @pl.when(has_next)
    def _():
        place(gh[...], halo, body, 2 * R * W)

    for side, ref, row in ((has_low, gd, 0), (has_high, gu, R + 1)):

        @pl.when(side)
        def _():
            place(ref[own], own, row, F * W)

        @pl.when(both(side, has_next))
        def _():
            place(ref[halo], halo, row, 2 * W)

    for f in range(F):
        yb[f] = shift_sum(backward(qq, w_one, f, range(3)), WW, C).astype(bf16).reshape(R, WW, C)
        for d in sorted(range(1, Z), key=lambda d: -abs(2 * d - Z)):
            b_out[d, f].start()

    for d in range(1, Z):
        y_own[d].wait()
    for d in range(Z):
        y_next[d].wait()
    chunks = []
    for m in range(Z):
        head = rf[m, two].astype(f32) + rp[m].astype(f32)
        if F > 2:
            head = jnp.concatenate([head, rf[m, pl.ds(2, F - 2)].astype(f32)], axis=0)
        chunks.append(head.reshape(rows, O))
    branch = jnp.concatenate(chunks, axis=1)
    source = latent[...].reshape(rows, C).astype(f32)
    out[...] = (source + branch).astype(bf16).reshape(F, R, W, C)

    grad_one = yb[:, :, block(z)].astype(f32)
    for d in range(1, Z):
        for f in range(F):
            b_out[d, f].wait()
        grad_one = grad_one + rb[d].astype(f32)
    grad_one = grad_one.reshape(rows, C)
    normed_one, inverse_one = normalize(source, g_one)
    grad = norm_backward(source, inverse_one, g_one, grad_one * silu_slope(normed_one))
    upstream = cotangent[...].reshape(rows, C).astype(f32)
    latent_grad[...] = (upstream + grad).astype(bf16).reshape(F, R, W, C)
    links.drain()


def local(sizes, latent, cotangent, gain_one, gain_two, kernel_one, kernel_two):
    S, Q, Z = sizes
    F, R, W, C = latent.shape
    O = kernel_one.shape[3]
    WW = W * Z
    OP = -(-O // 128) * 128
    rows = F * R * W
    taps = kernel_one.shape[:3]
    packed = (F, R, W, C)
    slots = 128
    shapes = [
        kernel_one.shape,
        kernel_two.shape,
        taps + (O, Z * OP),
        packed,
        (F, R + 2, WW, C),
        (Z, F, R, W, O),
        (F + 2, R + 2, WW, O),
        (Z,) + packed,
        (Z,) + packed,
        (2, R, W, C),
        (2, R, W, C),
        (Z,) + packed,
        None,
        None,
        (Z, F, R + 2, WW, OP),
        packed,
        (2, R, W, C),
        (F + 2, W, C),
        (F + 2, W, C),
        (F + 2, R + 2, WW, OP),
        (F + 2, R, WW, O),
        (Z, F, R, W, O),
        (Z, 2, R, W, O),
        (F, R, WW, C),
        (Z,) + packed,
        None,
    ]
    scratch = [pltpu.VMEM(shape, bf16) if shape else None for shape in shapes]
    scratch[12] = pltpu.VMEM((2, Z, 8, rows), f32)
    scratch[13] = pltpu.VMEM((Z, 8, C), f32)
    scratch[25] = pltpu.VMEM((8, 128), f32)
    vmem = pl.BlockSpec(memory_space=pltpu.VMEM)
    hbm = pl.BlockSpec(memory_space=pl.ANY)
    return pl.pallas_call(
        functools.partial(kernel, sizes),
        out_shape=[jax.ShapeDtypeStruct((F, R, W, C), bf16)] * 2,
        in_specs=[vmem, vmem, vmem, vmem, hbm, hbm],
        out_specs=[vmem, vmem],
        scratch_shapes=[
            *scratch,
            pltpu.SemaphoreType.DMA((slots,)),
            pltpu.SemaphoreType.DMA((slots,)),
            pltpu.SemaphoreType.DMA((2,)),
        ],
        compiler_params=pltpu.CompilerParams(
            collective_id=0, has_side_effects=True, vmem_limit_bytes=60 * 1024 * 1024
        ),
    )(latent, cotangent, gain_one, gain_two, kernel_one, kernel_two)


def solution(mesh):
    sizes = (mesh.shape["section"], mesh.shape["seq"], mesh.shape["exp"])
    spread = P("section", "seq", "exp", None)
    split = P(None, None, None, "exp", None)
    return jax.shard_map(
        functools.partial(local, sizes),
        mesh=mesh,
        in_specs=(spread, spread, P(), P(), split, split),
        out_specs=(spread, spread),
        check_vma=False,
    )
```

time: 73 us -> 61.7 us (0.85)
  Pallas kernels: 69.1 us -> 57.8 us
    pallas_call x1, Pallas kernels: 69.1 us -> 57.8 us  [local(): pl.pallas_call(functools.partial(kernel, sizes), out_shape=[jax.ShapeDtyp...]
where the time goes in v1:
time: 61.7 us; the launch traced here: 61.5 us
  Pallas kernels  57.8 us (94%)
  local copies, waits for them, and re-layouts  3.09 us (5%)
  between operations  0.64 us (1%)
    pallas_call x1, Pallas kernels, local(): pl.pallas_call(functools.partial(kernel, sizes), out_shape=[jax.ShapeDtyp...  57.8 us
    unnamed x2, local copies, waits for them, and re-layouts  3.09 us

profile of v1, /device:TPU:0, one launch (start us, length us, event | category | flops | bytes accessed | tf_op | source)
XLA Modules:
  0.0 61.5 jit_solution(883916104090914260)
XLA Ops:
  0.6 57.8 %shard_map.77 = (bf16[2,4,16,384]{3,2,1,0:T(8,128)(2,1)}, bf16[2,4,16,384]{3,2,1,0:T(8,128)(2,1)}) custom-call(bf16[2,4,16,384]{3,2,1,0:T(8,128)(2,1)} %latent.1, bf16[2,4,16,384]{3,2,1,0:T(8,128)(2,1)} %cotangent.1, f32[384]{0:T(512)} %gain_one.1, f32[384]{0:T(512)} %gain_two.1, bf16[3,3,3,96,384]{4,3,2,1,0:T(8,128)(2,1)} %kernel_one.1, ...), custom_call_target="tpu_custom_call" | custom-call | tf_op jit(solution)/shard_map/pallas_call | solution.py:562
  58.4 1.5 %copy.10 = bf16[2,4,16,384]{3,2,1,0:T(8,128)(2,1)} copy(bf16[2,4,16,384]{3,2,1,0:T(8,128)(2,1)} %get-tuple-element.4) | data formatting | bytes 196608
  60.0 1.5 %copy.11 = bf16[2,4,16,384]{3,2,1,0:T(8,128)(2,1)} copy(bf16[2,4,16,384]{3,2,1,0:T(8,128)(2,1)} %get-tuple-element.5) | data formatting | bytes 196608

commit v2 on v1

--- a/solution.py
+++ b/solution.py
@@ -43,6 +43,10 @@
         + jnp.where(column == 0, 0.0, low)
         + jnp.where(column == width - 1, 0.0, high)
     )
+
+
+def fold_of(rows, width):
+    return next((n for n in (4, 2) if rows % n == 0 and n * width % 128 == 0), 1)
 
 
 def pad_to(value, axis, size):
@@ -96,13 +100,14 @@
         pl.when(condition)(action)
 
 
-def kernel(sizes, latent, cotangent, gain_one, gain_two, kernel_one, kernel_two, out, latent_grad, *scratch):
+def kernel(sizes, latent_hbm, cotangent_hbm, gain_one_hbm, gain_two_hbm, kernel_one, kernel_two, out_hbm, latent_grad_hbm, *scratch):
     S, Q, Z = sizes
     (
         w_one, w_two, w_gap, act, xp, qs, qp, gs, gr, fs, fr, vall, st, gains,
-        xq, gi, gh, gu, gd, qq, yf, rf, rp, yb, rb, g_sum, send, recv, w_sem,
+        xq, gi, gh, gu, gd, qq, yf, rf, ys, yr, yb, rb, g_hop, b_hop,
+        latent, cotangent, gain_one, gain_two, out, latent_grad, send, recv, w_sem,
     ) = scratch
-    F, R, W, C = latent.shape
+    F, R, W, C = latent_hbm.shape
     O = kernel_one.shape[3]
     WW = W * Z
     OP = -(-O // 128) * 128
@@ -113,16 +118,32 @@
     both = jnp.logical_and
     nxt, prv = jnp.minimum(s + 1, S - 1), jnp.maximum(s - 1, 0)
     upper, lower = jnp.minimum(q + 1, Q - 1), jnp.maximum(q - 1, 0)
+    fold = fold_of(R, O)
     body, own, halo = pl.ds(1, R), pl.ds(0, F), pl.ds(F, 2)
     two = pl.ds(0, 2)
     links = Links(send, recv)
 
-    load_one = pltpu.make_async_copy(kernel_one, w_one, w_sem.at[0])
-    load_two = pltpu.make_async_copy(kernel_two, w_two, w_sem.at[1])
-    load_two.start()
-    load_one.start()
-
     barrier = pltpu.get_barrier_semaphore()
+    loads = [
+        pltpu.make_async_copy(src, dst, w_sem.at[k])
+        for k, (src, dst) in enumerate(
+            [
+                (cotangent_hbm, cotangent),
+                (latent_hbm, latent),
+                (gain_one_hbm, gain_one),
+                (gain_two_hbm, gain_two),
+                (kernel_two, w_two),
+                (kernel_one, w_one),
+            ]
+        )
+    ]
+    load_two, load_one = loads[4:]
+    stores = [
+        pltpu.make_async_copy(out, out_hbm, w_sem.at[6]),
+        pltpu.make_async_copy(latent_grad, latent_grad_hbm, w_sem.at[7]),
+    ]
+    for load in loads[:4]:
+        load.start()
 
     def greet(device):
         pl.semaphore_signal(barrier, inc=1, device_id=device, device_id_type=MESH)
@@ -147,6 +168,9 @@
         @pl.when(side)
         def _():
             greet((s, q + move, z))
+
+    for load in loads[4:]:
+        load.start()
 
     def peer(d):
         return lax.rem(z + d + Z, Z)
@@ -189,6 +213,66 @@
                 if distance == d:
                     when(made.receives, functools.partial(use, owner))
 
+    class Scatter:
+        def __init__(self, at, landing, hop):
+            self.at, self.landing, self.hop, self.far, self.near = at, landing, hop, {}, {}
+            for sign in (1, -1):
+                for D in range(Z - 1, 0, -1):
+                    for f in range(F):
+                        target, origin = z + sign * D, z - sign * D
+                        sends = (z + D < Z) if sign > 0 else (z >= D)
+                        src = at(jnp.clip(target, 0, Z - 1), f)
+                        if D >= 3:
+                            before = (z >= 1) if sign > 0 else (z < Z - 1)
+                            further = (z + D <= Z) if sign > 0 else (z >= D - 1)
+                            self.far[sign, D, f] = links.copy(
+                                src, hop.at[int(sign > 0), D - 3, f], (s, q, jnp.clip(z + sign, 0, Z - 1)), sends, both(before, further)
+                            )
+                        else:
+                            receives = (z >= D) if sign > 0 else (z + D < Z)
+                            slot = 2 * (sign > 0) + D - 1
+                            self.near[sign, D, f] = links.copy(
+                                src, landing.at[slot, f], (s, q, jnp.clip(target, 0, Z - 1)), sends, receives
+                            )
+
+        def start(self, f):
+            for D in range(Z - 1, 0, -1):
+                for sign in (1, -1):
+                    made = self.far.get((sign, D, f)) or self.near[sign, D, f]
+                    joined = self.far.get((sign, D + 1, f))
+                    if joined is None:
+                        made.start()
+                    else:
+                        when(both(made.sends, jnp.logical_not(joined.receives)), lambda: made.made().start())
+
+        def join(self, f):
+            for D in range(Z - 1, 2, -1):
+                for sign in (1, -1):
+                    arrived = self.far[sign, D, f]
+                    onward = self.far.get((sign, D - 1, f)) or self.near[sign, D - 1, f]
+
+                    @pl.when(arrived.receives)
+                    def _():
+                        arrived.made().wait_recv()
+                        held = self.at(jnp.clip(z + sign * (D - 1), 0, Z - 1), f)
+                        total = held[...].astype(f32) + self.hop[int(sign > 0), D - 3, f].astype(f32)
+                        held[...] = total.astype(bf16)
+                        onward.made().start()
+
+        def total(self, own):
+            for D in (1, 2):
+                for sign in (1, -1):
+                    for f in range(F):
+                        if (sign, D, f) in self.near:
+                            self.near[sign, D, f].wait()
+            for D in (1, 2):
+                for sign in (1, -1):
+                    if (sign, D, 0) in self.near:
+                        made = self.near[sign, D, 0]
+                        term = self.landing[2 * (sign > 0) + D - 1].astype(f32)
+                        own = own + jnp.where(made.receives, term, 0.0)
+            return own
+
     q_own = {d: links.copy(qs.at[peer(d)], qp.at[own, body, block(z)], (s, q, peer(d))) for d in range(1, Z)}
     q_next = {
         d: links.copy(
@@ -214,9 +298,7 @@
         rows_out(xp.at[:, 1], xp.at[:, R + 1], (s, lower, z), -1),
     ]
     x_all = gather(act, lambda owner: xp.at[:, body, block(owner)])
-    g_out = {
-        (d, f): links.copy(gs.at[peer(d), f], gr.at[d, f], (s, q, peer(d))) for d in range(1, Z) for f in range(F)
-    }
+    g_out = Scatter(lambda owner, f: gs.at[owner, f], gr, g_hop)
     f_out = [links.copy(fs.at[t], fr.at[t], (nxt, q, z), has_next, has_prev) for t in range(2)]
     v_all = gather(vall.at[z], lambda owner: vall.at[owner])
     sums = [{d: links.copy(st.at[k, 0], st.at[k, d], (s, q, peer(d))) for d in range(1, Z)} for k in range(2)]
@@ -233,16 +315,9 @@
         links.copy(gi.at[two, R - 1], gd.at[halo], (prv, upper, z), both(has_prev, has_high), both(has_next, has_low)),
         links.copy(gi.at[two, 0], gu.at[halo], (prv, lower, z), both(has_prev, has_low), both(has_next, has_high)),
     ]
-    b_out = {
-        (d, f): links.copy(yb.at[f, :, block(peer(d))], rb.at[d, f], (s, q, peer(d)))
-        for d in range(1, Z)
-        for f in range(F)
-    }
-    y_own = {d: links.copy(yf.at[own, :, block(peer(d))], rf.at[z], (s, q, peer(d))) for d in range(1, Z)}
-    y_next = {
-        d: links.copy(yf.at[halo, :, block(peer(d))], rp.at[z], (nxt, q, peer(d)), has_next, has_prev)
-        for d in range(Z)
-    }
+    b_out = Scatter(lambda owner, f: yb.at[f, :, block(owner)], rb, b_hop)
+    y_own = {d: links.copy(yf.at[peer(d)], rf.at[z], (s, q, peer(d))) for d in range(1, Z)}
+    y_next = [links.copy(ys.at[t], yr.at[t], (nxt, q, z), has_next, has_prev) for t in range(2)]
 
     lane = lax.broadcasted_iota(jnp.int32, (8, C), 1)
     group = lax.broadcasted_iota(jnp.int32, (8, C), 0)
@@ -297,12 +372,15 @@
             total = part if total is None else total + part
         return total
 
+    loads[0].wait()
+    for m in range(Z):
+        qs[m] = cotangent[:, :, :, m * O : (m + 1) * O]
+    for load in loads[1:4]:
+        load.wait()
     source = latent[...].reshape(rows, C).astype(f32)
     g_one, g_two = gain_one[...].reshape(1, C), gain_two[...].reshape(1, C)
     normed_one, _ = normalize(source, g_one)
     act[...] = silu(normed_one).astype(bf16).reshape(F, R, W, C)
-    for m in range(Z):
-        qs[m] = cotangent[:, :, :, m * O : (m + 1) * O]
 
     near = has_next.astype(jnp.int32) + has_prev.astype(jnp.int32)
     sides = has_high.astype(jnp.int32) + has_low.astype(jnp.int32)
@@ -337,17 +415,11 @@
     @pl.when(jnp.logical_not(has_prev))
     def _():
         zero(fr, (full,))
-        zero(rp, (full,))
+        zero(yr, (full,))
 
     for m in range(Z):
         gains[m] = jnp.broadcast_to(jnp.concatenate([g_two[:, m * O : (m + 1) * O]] * Z, axis=1), (8, C))
 
-    for d in range(1, Z):
-        q_own[d].wait()
-        q_next[d].start()
-    for made in q_rows + q_corner:
-        made.start()
-    gather_wait(x_all, 2)
     load_two.wait()
     for i in range(3):
         for j in range(3):
@@ -356,18 +428,25 @@
                 w_gap[i, j, l] = jnp.concatenate(
                     [pad_to(w[:, m * O : (m + 1) * O], 1, OP) for m in range(Z)], axis=1
                 ).astype(bf16)
+    for d in range(1, Z):
+        q_own[d].wait()
+        q_next[d].start()
+    for made in q_rows + q_corner:
+        made.start()
     for made in q_rows:
         made.wait()
+    early = [backward(qp, w_two, f, range(F - f)) for f in range(F)]
+    gather_wait(x_all, 2)
     for d in range(Z):
         q_next[d].wait()
     for made in q_corner:
         made.wait()
     for f in range(F):
-        total = shift_sum(backward(qp, w_two, f, range(3)), WW, C)
+        total = early[f] + backward(qp, w_two, f, range(F - f, 3))
+        total = shift_sum(total, WW, C)
         for m in range(Z):
             gs[m, f] = pack(total, m * O).astype(bf16).reshape(R, W, C)
-        for d in sorted(range(1, Z), key=lambda d: -abs(2 * d - Z)):
-            g_out[d, f].start()
+        g_out.start(f)
 
     gather_wait(x_all, 1)
     for d in range(3, Z):
@@ -385,6 +464,8 @@
         fs[t - F] = pack(forward(lhs_one, w_one, t)).astype(bf16).reshape(R, W, C)
         f_out[t - F].start()
     inner = [pack(forward(lhs_one, w_one, t)) for t in range(F)]
+    for f in range(F):
+        g_out.join(f)
     for made in f_out:
         made.wait()
     for t in range(2):
@@ -394,14 +475,9 @@
     st[0, 0] = segment_sums(inner * inner)
     for d in range(1, Z):
         sums[0][d].start()
+
+    grad_two = g_out.total(gs[z].astype(f32)).reshape(rows, C)
     gather_start(v_all)
-
-    grad_two = gs[z].astype(f32)
-    for d in range(1, Z):
-        for f in range(F):
-            g_out[d, f].wait()
-        grad_two = grad_two + gr[d].astype(f32)
-    grad_two = grad_two.reshape(rows, C)
     squares = st[0, 0]
     for d in range(1, Z):
         sums[0][d].wait()
@@ -443,76 +519,97 @@
                 qq.at[frames, band, m * W : (m + 1) * W].shape
             )
 
+    place(gi[...], own, body, rows)
     for d in range(3, Z):
         gather_wait(v_all, d, activate)
     for made in xq_rows:
         made.start()
-    place(gi[...], own, body, rows)
-    for made in xq_rows:
-        made.wait()
+
+    def place_rows(frames, count, among):
+        for side, ref, row in ((has_low, gd, 0), (has_high, gu, R + 1)):
+
+            @pl.when(side if among is None else both(side, among))
+            def _():
+                place(ref[frames], frames, row, count * W)
+
+    for made in gi_rows:
+        made.wait()
+    place_rows(own, F, None)
+
+    early = [backward(qq, w_one, f, range(F - f)) for f in range(F)]
 
     def lhs_two(f):
         return jnp.concatenate(
             [xq[m, f, pl.ds(j, R)].reshape(R * WW, OP) for j in range(3) for m in range(Z)], axis=1
         )
 
-    for t in (F, F + 1):
-        yf[t] = forward(lhs_two, w_gap, t).astype(bf16).reshape(R, WW, O)
-    for d in range(Z):
-        y_next[d].start()
-    for t in range(F):
-        yf[t] = forward(lhs_two, w_gap, t).astype(bf16).reshape(R, WW, O)
-    for d in range(1, Z):
-        y_own[d].start()
-    rf[z] = yf[own, :, block(z)]
-
-    for made in gi_rows + gi_corner + [gi_next]:
+    for made in xq_rows:
+        made.wait()
+    for t in (F + 1, F):
+        ys[t - F] = pack(forward(lhs_two, w_gap, t)).astype(bf16).reshape(R, W, C)
+        y_next[t - F].start()
+    for made in gi_corner + [gi_next]:
         made.wait()
 
     @pl.when(has_next)
     def _():
         place(gh[...], halo, body, 2 * R * W)
 
-    for side, ref, row in ((has_low, gd, 0), (has_high, gu, R + 1)):
-
-        @pl.when(side)
-        def _():
-            place(ref[own], own, row, F * W)
-
-        @pl.when(both(side, has_next))
-        def _():
-            place(ref[halo], halo, row, 2 * W)
-
+    place_rows(halo, 2, has_next)
     for f in range(F):
-        yb[f] = shift_sum(backward(qq, w_one, f, range(3)), WW, C).astype(bf16).reshape(R, WW, C)
-        for d in sorted(range(1, Z), key=lambda d: -abs(2 * d - Z)):
-            b_out[d, f].start()
+        total = early[f] + backward(qq, w_one, f, range(F - f, 3))
+        yb[f] = shift_sum(total, WW, C).astype(bf16).reshape(R, WW, C)
+        b_out.start(f)
+    branch = [forward(lhs_two, w_gap, t).reshape(R, Z, W, O) for t in range(F)]
+    for made in y_next:
+        made.wait()
+    for t in range(F):
+        for m in range(Z):
+            term = branch[t][:, m].reshape(R // fold, fold, W, O)
+            if t < 2:
+                carried = yr[t].reshape(R * W, C).astype(f32)[:, m * O : (m + 1) * O]
+                term = term + carried.reshape(R // fold, fold, W, O)
+            yf[m, t] = jnp.concatenate(
+                [term[:, k].reshape(R // fold * W, O) for k in range(fold)], axis=1
+            ).astype(bf16).reshape(R // fold, W, fold * O)
+    for d in sorted(range(1, Z), key=lambda d: -abs(2 * d - Z)):
+        y_own[d].start()
+    rf[z] = yf[z]
+    for f in range(F):
+        b_out.join(f)
 
     for d in range(1, Z):
         y_own[d].wait()
-    for d in range(Z):
-        y_next[d].wait()
     chunks = []
     for m in range(Z):
-        head = rf[m, two].astype(f32) + rp[m].astype(f32)
-        if F > 2:
-            head = jnp.concatenate([head, rf[m, pl.ds(2, F - 2)].astype(f32)], axis=0)
-        chunks.append(head.reshape(rows, O))
+        value = rf[m].reshape(F * R // fold, W, fold * O).astype(f32)
+        parts = [value[:, :, k * O : (k + 1) * O] for k in range(fold)]
+        chunks.append(jnp.stack(parts, axis=1).reshape(rows, O))
     branch = jnp.concatenate(chunks, axis=1)
     source = latent[...].reshape(rows, C).astype(f32)
     out[...] = (source + branch).astype(bf16).reshape(F, R, W, C)
-
-    grad_one = yb[:, :, block(z)].astype(f32)
-    for d in range(1, Z):
-        for f in range(F):
-            b_out[d, f].wait()
-        grad_one = grad_one + rb[d].astype(f32)
-    grad_one = grad_one.reshape(rows, C)
+    stores[0].start()
+
+    grad_one = b_out.total(yb[:, :, block(z)].astype(f32)).reshape(rows, C)
     normed_one, inverse_one = normalize(source, g_one)
     grad = norm_backward(source, inverse_one, g_one, grad_one * silu_slope(normed_one))
     upstream = cotangent[...].reshape(rows, C).astype(f32)
     latent_grad[...] = (upstream + grad).astype(bf16).reshape(F, R, W, C)
+    stores[1].start()
     links.drain()
+    for store in stores:
+        store.wait()
+
+
+def hand_over(first, second, first_out, second_out, sem):
+    copies = [
+        pltpu.make_async_copy(first, first_out, sem.at[0]),
+        pltpu.make_async_copy(second, second_out, sem.at[1]),
+    ]
+    for made in copies:
+        made.start()
+    for made in copies:
+        made.wait()
 
 
 def local(sizes, latent, cotangent, gain_one, gain_two, kernel_one, kernel_two):
@@ -523,6 +620,7 @@
     OP = -(-O // 128) * 128
     rows = F * R * W
     taps = kernel_one.shape[:3]
+    fold = fold_of(R, O)
     packed = (F, R, W, C)
     slots = 128
     shapes = [
@@ -534,7 +632,7 @@
         (Z, F, R, W, O),
         (F + 2, R + 2, WW, O),
         (Z,) + packed,
-        (Z,) + packed,
+        (4,) + packed,
         (2, R, W, C),
         (2, R, W, C),
         (Z,) + packed,
@@ -546,35 +644,53 @@
         (F + 2, W, C),
         (F + 2, W, C),
         (F + 2, R + 2, WW, OP),
-        (F + 2, R, WW, O),
-        (Z, F, R, W, O),
-        (Z, 2, R, W, O),
+        (Z, F, R // fold, W, fold * O),
+        (Z, F, R // fold, W, fold * O),
+        (2, R, W, C),
+        (2, R, W, C),
         (F, R, WW, C),
-        (Z,) + packed,
+        (4,) + packed,
+        (2, max(Z - 3, 1)) + packed,
+        (2, max(Z - 3, 1)) + packed,
+        packed,
+        packed,
         None,
+        None,
+        packed,
+        packed,
     ]
     scratch = [pltpu.VMEM(shape, bf16) if shape else None for shape in shapes]
     scratch[12] = pltpu.VMEM((2, Z, 8, rows), f32)
     scratch[13] = pltpu.VMEM((Z, 8, C), f32)
-    scratch[25] = pltpu.VMEM((8, 128), f32)
-    vmem = pl.BlockSpec(memory_space=pltpu.VMEM)
-    hbm = pl.BlockSpec(memory_space=pl.ANY)
-    return pl.pallas_call(
+    scratch[30] = scratch[31] = pltpu.VMEM((C,), f32)
+    hbm = pl.BlockSpec(memory_space=pltpu.HBM)
+    results = pl.pallas_call(
         functools.partial(kernel, sizes),
         out_shape=[jax.ShapeDtypeStruct((F, R, W, C), bf16)] * 2,
-        in_specs=[vmem, vmem, vmem, vmem, hbm, hbm],
-        out_specs=[vmem, vmem],
+        in_specs=[hbm] * 6,
+        out_specs=[hbm] * 2,
         scratch_shapes=[
             *scratch,
             pltpu.SemaphoreType.DMA((slots,)),
             pltpu.SemaphoreType.DMA((slots,)),
-            pltpu.SemaphoreType.DMA((2,)),
+            pltpu.SemaphoreType.DMA((8,)),
         ],
         compiler_params=pltpu.CompilerParams(
             collective_id=0, has_side_effects=True, vmem_limit_bytes=60 * 1024 * 1024
         ),
     )(latent, cotangent, gain_one, gain_two, kernel_one, kernel_two)
-
+    vmem = pl.BlockSpec(memory_space=pltpu.VMEM)
+
+    def pass_on(first, second, first_out, second_out):
+        first_out[...] = first[...]
+        second_out[...] = second[...]
+
+    return pl.pallas_call(
+        pass_on,
+        out_shape=[jax.ShapeDtypeStruct((F, R, W, C), bf16)] * 2,
+        in_specs=[vmem] * 2,
+        out_specs=[vmem] * 2,
+    )(*results)
 
 def solution(mesh):
     sizes = (mesh.shape["section"], mesh.shape["seq"], mesh.shape["exp"])

time: 61.7 us -> 56.9 us (0.922)
  local copies, waits for them, and re-layouts: 3.09 us -> 0 us
  Pallas kernels: 57.8 us -> 56.1 us
    pallas_call x1, Pallas kernels: 57.8 us -> 54.5 us  [local(): pl.pallas_call(functools.partial(kernel, sizes), out_shape=[jax.ShapeDtyp...]
    unnamed x2 -> x0, local copies, waits for them, and re-layouts: 3.09 us -> none
    pallas_call x0 -> x1, Pallas kernels: none -> 1.62 us  [local(): pl.pallas_call(pass_on, out_shape=[jax.ShapeDtypeStruct((F, R, W, C), bf1...]
where the time goes in v2:
time: 56.9 us; the launch traced here: 56.7 us
  Pallas kernels  56.1 us (99%)
  between operations  0.64 us (1%)
    pallas_call x1, Pallas kernels, local(): pl.pallas_call(functools.partial(kernel, sizes), out_shape=[jax.ShapeDtyp...  54.5 us
    pallas_call x1, Pallas kernels, local(): pl.pallas_call(pass_on, out_shape=[jax.ShapeDtypeStruct((F, R, W, C), bf1...  1.62 us

profile of v2, /device:TPU:0, one launch (start us, length us, event | category | flops | bytes accessed | tf_op | source)
XLA Modules:
  0.0 56.7 jit_solution(6090173153747101680)
XLA Ops:
  0.6 54.5 %shard_map.77 = (bf16[2,4,16,384]{3,2,1,0:T(8,128)(2,1)}, bf16[2,4,16,384]{3,2,1,0:T(8,128)(2,1)}) custom-call(bf16[2,4,16,384]{3,2,1,0:T(8,128)(2,1)} %latent_hbm.1, bf16[2,4,16,384]{3,2,1,0:T(8,128)(2,1)} %cotangent_hbm.1, f32[384]{0:T(512)} %gain_one_hbm.1, f32[384]{0:T(512)} %gain_two_hbm.1, bf16[3,3,3,96,384]{4,3,2,1,0:T(8,128)(2,1)} %kernel_one.1, ...), custom_call_target="tpu_custom_call" | custom-call | tf_op jit(solution)/shard_map/pallas_call | solution.py:667
  55.1 1.6 %shard_map.78 = (bf16[2,4,16,384]{3,2,1,0:T(8,128)(2,1)}, bf16[2,4,16,384]{3,2,1,0:T(8,128)(2,1)}) custom-call(bf16[2,4,16,384]{3,2,1,0:T(8,128)(2,1)} %get-tuple-element.4.first, bf16[2,4,16,384]{3,2,1,0:T(8,128)(2,1)} %get-tuple-element.5.second), custom_call_target="tpu_custom_call" | custom-call | tf_op jit(solution)/shard_map/pallas_call | solution.py:688

commit v3 on v2

--- a/solution.py
+++ b/solution.py
@@ -69,6 +69,7 @@
     def drain(self):
         for made in self.all:
             made.drain()
+        assert len(self.all) == self.send.shape[0], len(self.all)
 
 
 class Copy:
@@ -103,9 +104,9 @@
 def kernel(sizes, latent_hbm, cotangent_hbm, gain_one_hbm, gain_two_hbm, kernel_one, kernel_two, out_hbm, latent_grad_hbm, *scratch):
     S, Q, Z = sizes
     (
-        w_one, w_two, w_gap, act, xp, qs, qp, gs, gr, fs, fr, vall, st, gains,
-        xq, gi, gh, gu, gd, qq, yf, rf, ys, yr, yb, rb, g_hop, b_hop,
-        latent, cotangent, gain_one, gain_two, out, latent_grad, send, recv, w_sem,
+        w_one, w_two, w_gap, act, xp, qs, qr, qn, qp, gs, gr, fs, fr, vall, st, gains,
+        xq, gi, gh, gu, gd, qq, yf, rf, ys, yr, yb, rb, g_hop, b_hop, vh, gt, sq, sh, early,
+        latent, cotangent, gain_one, gain_two, out, latent_grad, send, recv, w_sem, seen,
     ) = scratch
     F, R, W, C = latent_hbm.shape
     O = kernel_one.shape[3]
@@ -148,14 +149,18 @@
     def greet(device):
         pl.semaphore_signal(barrier, inc=1, device_id=device, device_id_type=MESH)
 
-    for d in range(1, Z):
-        greet((s, q, lax.rem(z + d, Z)))
+    has_right, has_left = z < Z - 1, z > 0
+    for beside, step in ((has_right, 1), (has_left, -1)):
+
+        @pl.when(beside)
+        def _():
+            greet((s, q, z + step))
+
     for near, step in ((has_next, 1), (has_prev, -1)):
 
         @pl.when(near)
         def _():
-            for d in range(Z):
-                greet((s + step, q, lax.rem(z + d, Z)))
+            greet((s + step, q, z))
 
         for side, move in ((has_high, 1), (has_low, -1)):
 
@@ -178,11 +183,11 @@
     def block(index):
         return pl.ds(pl.multiple_of(index * W, W), W)
 
-    def gather(source, at):
+    def gather(source, at, reach):
         arrive = []
         for d in range(1, Z):
             for sign in (1, -1):
-                if d <= 2:
+                if d <= reach:
                     target, sends = z + sign * d, (z + d < Z) if sign > 0 else (z >= d)
                     src, dst = source, at(z)
                 else:
@@ -195,18 +200,18 @@
                 arrive.append((d, z - sign * d, links.copy(src, dst, (s, q, target), sends, receives)))
         return arrive
 
-    def gather_start(arrive):
-        for d in (2, 1):
+    def gather_start(arrive, distances):
+        for d in distances:
             for distance, _, made in arrive:
                 if distance == d:
                     made.start()
 
-    def gather_wait(arrive, d, use=None):
+    def gather_wait(arrive, d, reach, use=None):
         for distance, owner, made in arrive:
             if distance == d:
                 made.wait()
         for distance, owner, made in arrive:
-            if distance == d + 1 and d >= 2:
+            if distance == d + 1 and d >= reach:
                 made.start()
         if use is not None:
             for distance, owner, made in arrive:
@@ -235,8 +240,8 @@
                                 src, landing.at[slot, f], (s, q, jnp.clip(target, 0, Z - 1)), sends, receives
                             )
 
-        def start(self, f):
-            for D in range(Z - 1, 0, -1):
+        def start(self, f, distances):
+            for D in distances:
                 for sign in (1, -1):
                     made = self.far.get((sign, D, f)) or self.near[sign, D, f]
                     joined = self.far.get((sign, D + 1, f))
@@ -273,13 +278,24 @@
                         own = own + jnp.where(made.receives, term, 0.0)
             return own
 
-    q_own = {d: links.copy(qs.at[peer(d)], qp.at[own, body, block(z)], (s, q, peer(d))) for d in range(1, Z)}
+    q_own = {}
+    for d in range(1, Z):
+        for sign in (1, -1):
+            target = jnp.clip(z + sign * d, 0, Z - 1)
+            ends = (z + d < Z, z >= d)
+            q_own[sign, d] = links.copy(qs.at[target], qr.at[z], (s, q, target), *ends[::sign])
     q_next = {
-        d: links.copy(
-            qp.at[two, body, block(peer(-d))], qp.at[halo, body, block(peer(-d))], (prv, q, z), has_prev, has_next
-        )
+        d: links.copy((qr if d else qs).at[peer(-d), two], qn.at[peer(-d)], (prv, q, z), has_prev, has_next)
         for d in range(Z)
     }
+
+    def q_pass_on(sign, d):
+        made = q_own[sign, d]
+        made.wait()
+
+        @pl.when(made.receives)
+        def _():
+            q_next[(sign * d) % Z].start()
 
     def rows_out(src, dst, device, towards):
         sides = (has_high, has_low) if towards > 0 else (has_low, has_high)
@@ -297,24 +313,27 @@
         rows_out(xp.at[:, R], xp.at[:, 0], (s, upper, z), 1),
         rows_out(xp.at[:, 1], xp.at[:, R + 1], (s, lower, z), -1),
     ]
-    x_all = gather(act, lambda owner: xp.at[:, body, block(owner)])
+    x_all = gather(act, lambda owner: xp.at[:, body, block(owner)], Z)
     g_out = Scatter(lambda owner, f: gs.at[owner, f], gr, g_hop)
     f_out = [links.copy(fs.at[t], fr.at[t], (nxt, q, z), has_next, has_prev) for t in range(2)]
-    v_all = gather(vall.at[z], lambda owner: vall.at[owner])
+    v_all = gather(vall.at[z], lambda owner: vall.at[owner], 2)
     sums = [{d: links.copy(st.at[k, 0], st.at[k, d], (s, q, peer(d))) for d in range(1, Z)} for k in range(2)]
     xq_rows = [
         rows_out(xq.at[:, :, R], xq.at[:, :, 0], (s, upper, z), 1),
         rows_out(xq.at[:, :, 1], xq.at[:, :, R + 1], (s, lower, z), -1),
     ]
-    gi_next = links.copy(gi.at[two], gh, (prv, q, z), has_prev, has_next)
-    gi_rows = [
-        rows_out(gi.at[:, R - 1], gd.at[own], (s, upper, z), 1),
-        rows_out(gi.at[:, 0], gu.at[own], (s, lower, z), -1),
-    ]
-    gi_corner = [
-        links.copy(gi.at[two, R - 1], gd.at[halo], (prv, upper, z), both(has_prev, has_high), both(has_next, has_low)),
-        links.copy(gi.at[two, 0], gu.at[halo], (prv, lower, z), both(has_prev, has_low), both(has_next, has_high)),
-    ]
+    v_next = links.copy(vall.at[z, two], vh, (prv, q, z), has_prev, has_next)
+    g_next = links.copy(gt, gh, (prv, q, z), has_prev, has_next)
+    squares_next = links.copy(sq, sh.at[Z], (prv, q, z), has_prev, has_next)
+    sums_next = {d: links.copy(st.at[1, 0], sh.at[d], (prv, q, peer(d)), has_prev, has_next) for d in range(Z)}
+
+    def gi_out(frames):
+        return [
+            rows_out(gi.at[frames, R - 1], gd.at[frames], (s, upper, z), 1),
+            rows_out(gi.at[frames, 0], gu.at[frames], (s, lower, z), -1),
+        ]
+
+    gi_rows, gi_corner = gi_out(own), gi_out(halo)
     b_out = Scatter(lambda owner, f: yb.at[f, :, block(owner)], rb, b_hop)
     y_own = {d: links.copy(yf.at[peer(d)], rf.at[z], (s, q, peer(d))) for d in range(1, Z)}
     y_next = [links.copy(ys.at[t], yr.at[t], (nxt, q, z), has_next, has_prev) for t in range(2)]
@@ -339,9 +358,13 @@
     def spread(tile):
         return lax.dot_general(tile, segments, (((0,), (0,)), ((), ())), precision=EXACT, preferred_element_type=f32)
 
-    def rhs_forward(w, i, K):
+    def rhs_forward(w, taps):
         return jnp.concatenate(
-            [jnp.concatenate([pad_to(w[i, j, l], 0, OP) for l in range(3)], axis=0) for j in range(3)], axis=1
+            [
+                jnp.concatenate([pad_to(w[i, j, l], 0, OP) for l in range(3) for i in taps], axis=0)
+                for j in range(3)
+            ],
+            axis=1,
         )
 
     def rhs_backward(w, i):
@@ -350,31 +373,58 @@
             axis=0,
         )
 
-    def forward(lhs_of, w, t):
-        total = None
-        for i in range(3):
-            f = t + i - 2
-            if not 0 <= f < F:
-                continue
-            part = lax.dot_general(
-                lhs_of(f), rhs_forward(w, i, None), (((1,), (1,)), ((), ())), preferred_element_type=f32
+    def forward(lhs_of, w):
+        parts = {}
+
+        def run(f, taps):
+            product = lax.dot_general(
+                lhs_of(f), rhs_forward(w, taps), (((1,), (1,)), ((), ())), preferred_element_type=f32
             )
-            total = part if total is None else total + part
-        return shift_sum(total, WW, OP)[:, :O]
+            joined = shift_sum(product, WW, len(taps) * OP)
+            for n, i in enumerate(taps):
+                parts.setdefault(f + 2 - i, []).append(joined[:, n * OP : n * OP + O])
+
+        def finish(t):
+            return functools.reduce(lambda a, b: a + b, parts[t])
+
+        def ahead(t):
+            if not parts:
+                for f in range(F - 1, max(F - 3, -1), -1):
+                    run(f, (0, 1))
+            return finish(t)
+
+        def rest(t):
+            for f in range(F):
+                if f + 2 - 2 == t:
+                    run(f, (2,) if f >= F - 2 else (0, 1, 2))
+            return finish(t)
+
+        return ahead, rest
 
     def backward(qbuf, w, f, taps):
-        total = None
-        for i in taps:
-            lhs = jnp.concatenate(
-                [pad_to(qbuf[f + i, pl.ds(j, R)].reshape(R * WW, qbuf.shape[3]), 1, OP) for j in range(3)], axis=1
-            )
-            part = jnp.dot(lhs, rhs_backward(w, i), preferred_element_type=f32)
-            total = part if total is None else total + part
-        return total
+        lhs = jnp.concatenate(
+            [
+                pad_to(qbuf[f + i, pl.ds(j, R)].reshape(R * WW, qbuf.shape[3]), 1, OP)
+                for i in taps
+                for j in range(3)
+            ],
+            axis=1,
+        )
+        rhs = jnp.concatenate([rhs_backward(w, i) for i in taps], axis=0)
+        return jnp.dot(lhs, rhs, preferred_element_type=f32)
+
+    def fold_rows(pieces):
+        return jnp.concatenate([p.reshape(p.shape[0] * W, O) for p in pieces], axis=1).astype(bf16)
+
+    def unfold_rows(value, width):
+        value = value.reshape(value.shape[0] * value.shape[1], W, fold * O).astype(f32)
+        parts = [pad_to(value[:, :, k * O : (k + 1) * O], 2, width) for k in range(fold)]
+        return jnp.stack(parts, axis=1).reshape(-1, R, W, width)
 
     loads[0].wait()
+    folded = cotangent[...].astype(f32).reshape(F * R // fold, fold, W, C)
     for m in range(Z):
-        qs[m] = cotangent[:, :, :, m * O : (m + 1) * O]
+        qs[m] = fold_rows([folded[:, k, :, m * O : (m + 1) * O] for k in range(fold)]).reshape(qs.shape[1:])
     for load in loads[1:4]:
         load.wait()
     source = latent[...].reshape(rows, C).astype(f32)
@@ -384,12 +434,39 @@
 
     near = has_next.astype(jnp.int32) + has_prev.astype(jnp.int32)
     sides = has_high.astype(jnp.int32) + has_low.astype(jnp.int32)
-    pl.semaphore_wait(barrier, Z - 1 + Z * near + sides + near * sides)
-
-    for d in sorted(range(1, Z), key=lambda d: -abs(2 * d - Z)):
-        q_own[d].start()
-    gather_start(x_all)
-    qp[own, body, block(z)] = qs[z]
+    beside = has_right.astype(jnp.int32) + has_left.astype(jnp.int32)
+    pl.semaphore_wait(barrier, beside + near + sides + near * sides)
+
+    def announce(d):
+        for k, known, teller in (
+            (0, z + d - 1 < Z, has_left),
+            (1, z >= d - 1, has_right),
+        ):
+
+            @pl.when(both(known, teller))
+            def _():
+                pl.semaphore_signal(
+                    seen.at[k, d - 2],
+                    inc=1,
+                    device_id=(s, q, jnp.clip(z - 1 if k == 0 else z + 1, 0, Z - 1)),
+                    device_id_type=MESH,
+                )
+
+    def await_seen(d):
+        for k, known in ((0, z + d < Z), (1, z >= d)):
+
+            @pl.when(known)
+            def _():
+                pl.semaphore_wait(seen.at[k, d - 2], 1)
+
+    for d in range(1, Z):
+        if d > 1:
+            await_seen(d)
+        if d < Z - 1:
+            announce(d + 1)
+        for sign in (1, -1):
+            q_own[sign, d].start()
+    qr[z] = qs[z]
     xp[:, body, block(z)] = act[...]
     q_next[0].start()
 
@@ -428,17 +505,26 @@
                 w_gap[i, j, l] = jnp.concatenate(
                     [pad_to(w[:, m * O : (m + 1) * O], 1, OP) for m in range(Z)], axis=1
                 ).astype(bf16)
+    gather_start(x_all, range(Z - 1, 0, -1))
     for d in range(1, Z):
-        q_own[d].wait()
-        q_next[d].start()
+        for sign in (1, -1):
+            q_pass_on(sign, d)
+    for m in range(Z):
+        qp[own, body, m * W : (m + 1) * W] = unfold_rows(qr[m], OP).astype(bf16)
     for made in q_rows + q_corner:
         made.start()
     for made in q_rows:
         made.wait()
-    early = [backward(qp, w_two, f, range(F - f)) for f in range(F)]
-    gather_wait(x_all, 2)
+    for f in range(F):
+        early[f] = backward(qp, w_two, f, range(F - f))
     for d in range(Z):
         q_next[d].wait()
+
+    @pl.when(has_next)
+    def _():
+        for m in range(Z):
+            qp[halo, body, m * W : (m + 1) * W] = unfold_rows(qn[m], OP).astype(bf16)
+
     for made in q_corner:
         made.wait()
     for f in range(F):
@@ -446,11 +532,12 @@
         total = shift_sum(total, WW, C)
         for m in range(Z):
             gs[m, f] = pack(total, m * O).astype(bf16).reshape(R, W, C)
-        g_out.start(f)
-
-    gather_wait(x_all, 1)
-    for d in range(3, Z):
-        gather_wait(x_all, d)
+        g_out.start(f, range(Z - 1, 1, -1))
+    for f in range(F):
+        g_out.start(f, (1,))
+
+    for d in range(1, Z):
+        gather_wait(x_all, d, Z)
     for made in x_rows:
         made.start()
     load_one.wait()
@@ -460,12 +547,14 @@
     def lhs_one(f):
         return jnp.concatenate([xp[f, pl.ds(j, R)].reshape(R * WW, C) for j in range(3)], axis=1)
 
+    ahead, inner = forward(lhs_one, w_one)
     for t in (F + 1, F):
-        fs[t - F] = pack(forward(lhs_one, w_one, t)).astype(bf16).reshape(R, W, C)
+        fs[t - F] = pack(ahead(t)).astype(bf16).reshape(R, W, C)
         f_out[t - F].start()
-    inner = [pack(forward(lhs_one, w_one, t)) for t in range(F)]
-    for f in range(F):
-        g_out.join(f)
+    rest, inner = inner, []
+    for t in range(F):
+        g_out.join(t)
+        inner.append(pack(rest(t)))
     for made in f_out:
         made.wait()
     for t in range(2):
@@ -476,12 +565,17 @@
     for d in range(1, Z):
         sums[0][d].start()
 
+    gather_start(v_all, (2,))
+    v_next.start()
     grad_two = g_out.total(gs[z].astype(f32)).reshape(rows, C)
-    gather_start(v_all)
+    gt[...] = grad_two[: 2 * R * W].astype(bf16).reshape(2, R, W, C)
+    g_next.start()
     squares = st[0, 0]
     for d in range(1, Z):
         sums[0][d].wait()
         squares = squares + st[0, d]
+    sq[...] = squares
+    squares_next.start()
     inverse = lax.rsqrt(squares / C + epsilon)
     inverse_wide = spread(inverse)
     gain = gains[z][0:1]
@@ -489,6 +583,8 @@
     st[1, 0] = segment_sums(inner * scaled)
     for d in range(1, Z):
         sums[1][d].start()
+    for d in range(Z):
+        sums_next[d].start()
 
     def activate(owner):
         value = vall[owner].reshape(rows, C).astype(f32)
@@ -496,9 +592,9 @@
         for m in range(Z):
             xq[owner, :, body, m * W : (m + 1) * W] = unpack(active, m).astype(bf16).reshape(F, R, W, OP)
 
+    gather_start(v_all, (1,))
     activate(z)
-    gather_wait(v_all, 2, activate)
-    gather_wait(v_all, 1, activate)
+    gather_wait(v_all, 2, 2, activate)
 
     means = st[1, 0]
     for d in range(1, Z):
@@ -506,9 +602,8 @@
         means = means + st[1, d]
     factor = spread(inverse * inverse * inverse * means / C)
     grad_inner = (inverse_wide * scaled - inner * factor).astype(bf16)
-    gi[...] = grad_inner.reshape(F, R, W, C)
-    gi_next.start()
-    for made in gi_rows + gi_corner:
+    gi[own] = grad_inner.reshape(F, R, W, C)
+    for made in gi_rows:
         made.start()
 
     def place(ref, frames, band, count):
@@ -519,11 +614,7 @@
                 qq.at[frames, band, m * W : (m + 1) * W].shape
             )
 
-    place(gi[...], own, body, rows)
-    for d in range(3, Z):
-        gather_wait(v_all, d, activate)
-    for made in xq_rows:
-        made.start()
+    place(gi[own], own, body, rows)
 
     def place_rows(frames, count, among):
         for side, ref, row in ((has_low, gd, 0), (has_high, gu, R + 1)):
@@ -532,11 +623,51 @@
             def _():
                 place(ref[frames], frames, row, count * W)
 
+    for made in (v_next, g_next, squares_next):
+        made.wait()
+    for d in range(Z):
+        sums_next[d].wait()
+
+    @pl.when(has_next)
+    def _():
+        taken = slice(0, 2 * R * W)
+        inverse = lax.rsqrt(sh[Z] / C + epsilon)
+        mean = sh[0]
+        for d in range(1, Z):
+            mean = mean + sh[d]
+        value = vh[...].reshape(2 * R * W, C).astype(f32)
+        inverse_wide = spread(inverse)[taken]
+        upstream = gh[...].reshape(2 * R * W, C).astype(f32)
+        upstream = upstream * silu_slope(value * inverse_wide * gain) * gain
+        factor = spread(inverse * inverse * inverse * mean / C)[taken]
+        gi[halo] = (inverse_wide * upstream - value * factor).astype(bf16).reshape(2, R, W, C)
+        place(gi[halo], halo, body, 2 * R * W)
+
+    @pl.when(jnp.logical_not(has_next))
+    def _():
+        zero(gi, (halo,))
+
+    for made in gi_corner:
+        made.start()
+    gather_wait(v_all, 1, 2, activate)
+    for d in range(3, Z):
+        gather_wait(v_all, d, 2, activate)
+    for made in xq_rows:
+        made.start()
     for made in gi_rows:
         made.wait()
     place_rows(own, F, None)
-
-    early = [backward(qq, w_one, f, range(F - f)) for f in range(F)]
+    for f in range(F):
+        early[f] = backward(qq, w_one, f, range(F - f))
+    for made in gi_corner:
+        made.wait()
+    place_rows(halo, 2, has_next)
+    for f in range(F):
+        total = early[f] + backward(qq, w_one, f, range(F - f, 3))
+        yb[f] = shift_sum(total, WW, C).astype(bf16).reshape(R, WW, C)
+        b_out.start(f, range(Z - 1, 1, -1))
+    for f in range(F):
+        b_out.start(f, (1,))
 
     def lhs_two(f):
         return jnp.concatenate(
@@ -545,22 +676,14 @@
 
     for made in xq_rows:
         made.wait()
+    ahead, branch = forward(lhs_two, w_gap)
     for t in (F + 1, F):
-        ys[t - F] = pack(forward(lhs_two, w_gap, t)).astype(bf16).reshape(R, W, C)
+        ys[t - F] = pack(ahead(t)).astype(bf16).reshape(R, W, C)
         y_next[t - F].start()
-    for made in gi_corner + [gi_next]:
-        made.wait()
-
-    @pl.when(has_next)
-    def _():
-        place(gh[...], halo, body, 2 * R * W)
-
-    place_rows(halo, 2, has_next)
-    for f in range(F):
-        total = early[f] + backward(qq, w_one, f, range(F - f, 3))
-        yb[f] = shift_sum(total, WW, C).astype(bf16).reshape(R, WW, C)
-        b_out.start(f)
-    branch = [forward(lhs_two, w_gap, t).reshape(R, Z, W, O) for t in range(F)]
+    rest, branch = branch, []
+    for t in range(F):
+        b_out.join(t)
+        branch.append(rest(t).reshape(R, Z, W, O))
     for made in y_next:
         made.wait()
     for t in range(F):
@@ -569,22 +692,16 @@
             if t < 2:
                 carried = yr[t].reshape(R * W, C).astype(f32)[:, m * O : (m + 1) * O]
                 term = term + carried.reshape(R // fold, fold, W, O)
-            yf[m, t] = jnp.concatenate(
-                [term[:, k].reshape(R // fold * W, O) for k in range(fold)], axis=1
-            ).astype(bf16).reshape(R // fold, W, fold * O)
+            yf[m, t] = fold_rows([term[:, k] for k in range(fold)]).reshape(R // fold, W, fold * O)
     for d in sorted(range(1, Z), key=lambda d: -abs(2 * d - Z)):
         y_own[d].start()
     rf[z] = yf[z]
-    for f in range(F):
-        b_out.join(f)
 
     for d in range(1, Z):
         y_own[d].wait()
     chunks = []
     for m in range(Z):
-        value = rf[m].reshape(F * R // fold, W, fold * O).astype(f32)
-        parts = [value[:, :, k * O : (k + 1) * O] for k in range(fold)]
-        chunks.append(jnp.stack(parts, axis=1).reshape(rows, O))
+        chunks.append(unfold_rows(rf[m], O).reshape(rows, O))
     branch = jnp.concatenate(chunks, axis=1)
     source = latent[...].reshape(rows, C).astype(f32)
     out[...] = (source + branch).astype(bf16).reshape(F, R, W, C)
@@ -622,15 +739,17 @@
     taps = kernel_one.shape[:3]
     fold = fold_of(R, O)
     packed = (F, R, W, C)
-    slots = 128
+    slots = (Z - 1) * (9 + 4 * F) + 2 * Z + 19
     shapes = [
         kernel_one.shape,
         kernel_two.shape,
         taps + (O, Z * OP),
         packed,
         (F, R + 2, WW, C),
-        (Z, F, R, W, O),
-        (F + 2, R + 2, WW, O),
+        (Z, F, R // fold, W, fold * O),
+        (Z, F, R // fold, W, fold * O),
+        (Z, 2, R // fold, W, fold * O),
+        (F + 2, R + 2, WW, OP),
         (Z,) + packed,
         (4,) + packed,
         (2, R, W, C),
@@ -639,7 +758,7 @@
         None,
         None,
         (Z, F, R + 2, WW, OP),
-        packed,
+        (F + 2, R, W, C),
         (2, R, W, C),
         (F + 2, W, C),
         (F + 2, W, C),
@@ -652,6 +771,11 @@
         (4,) + packed,
         (2, max(Z - 3, 1)) + packed,
         (2, max(Z - 3, 1)) + packed,
+        (2, R, W, C),
+        (2, R, W, C),
+        None,
+        None,
+        None,
         packed,
         packed,
         None,
@@ -660,9 +784,12 @@
         packed,
     ]
     scratch = [pltpu.VMEM(shape, bf16) if shape else None for shape in shapes]
-    scratch[12] = pltpu.VMEM((2, Z, 8, rows), f32)
-    scratch[13] = pltpu.VMEM((Z, 8, C), f32)
-    scratch[30] = scratch[31] = pltpu.VMEM((C,), f32)
+    scratch[14] = pltpu.VMEM((2, Z, 8, rows), f32)
+    scratch[15] = pltpu.VMEM((Z, 8, C), f32)
+    scratch[32] = pltpu.VMEM((8, rows), f32)
+    scratch[33] = pltpu.VMEM((Z + 1, 8, rows), f32)
+    scratch[34] = pltpu.VMEM((F, R * WW, 3 * C), f32)
+    scratch[37] = scratch[38] = pltpu.VMEM((C,), f32)
     hbm = pl.BlockSpec(memory_space=pltpu.HBM)
     results = pl.pallas_call(
         functools.partial(kernel, sizes),
@@ -674,6 +801,7 @@
             pltpu.SemaphoreType.DMA((slots,)),
             pltpu.SemaphoreType.DMA((slots,)),
             pltpu.SemaphoreType.DMA((8,)),
+            pltpu.SemaphoreType.REGULAR((2, max(Z - 2, 1))),
         ],
         compiler_params=pltpu.CompilerParams(
             collective_id=0, has_side_effects=True, vmem_limit_bytes=60 * 1024 * 1024

time: 56.9 us -> 51.7 us (0.909)
  Pallas kernels: 56.1 us -> 50.9 us
    pallas_call x1, Pallas kernels: 54.5 us -> 49.3 us  [local(): pl.pallas_call(functools.partial(kernel, sizes), out_shape=[jax.ShapeDtyp...]
where the time goes in v3:
time: 51.7 us; the launch traced here: 51.5 us
  Pallas kernels  50.9 us (98%)
  between operations  0.64 us (1%)
    pallas_call x1, Pallas kernels, local(): pl.pallas_call(functools.partial(kernel, sizes), out_shape=[jax.ShapeDtyp...  49.3 us
    pallas_call x1, Pallas kernels, local(): pl.pallas_call(pass_on, out_shape=[jax.ShapeDtypeStruct((F, R, W, C), bf1...  1.62 us

profile of v3, /device:TPU:0, one launch (start us, length us, event | category | flops | bytes accessed | tf_op | source)
XLA Modules:
  0.0 51.5 jit_solution(3317044290855541678)
XLA Ops:
  0.6 49.3 %shard_map.77 = (bf16[2,4,16,384]{3,2,1,0:T(8,128)(2,1)}, bf16[2,4,16,384]{3,2,1,0:T(8,128)(2,1)}) custom-call(bf16[2,4,16,384]{3,2,1,0:T(8,128)(2,1)} %latent_hbm.1, bf16[2,4,16,384]{3,2,1,0:T(8,128)(2,1)} %cotangent_hbm.1, f32[384]{0:T(512)} %gain_one_hbm.1, f32[384]{0:T(512)} %gain_two_hbm.1, bf16[3,3,3,96,384]{4,3,2,1,0:T(8,128)(2,1)} %kernel_one.1, ...), custom_call_target="tpu_custom_call" | custom-call | tf_op jit(solution)/shard_map/pallas_call | solution.py:794
  49.9 1.6 %shard_map.78 = (bf16[2,4,16,384]{3,2,1,0:T(8,128)(2,1)}, bf16[2,4,16,384]{3,2,1,0:T(8,128)(2,1)}) custom-call(bf16[2,4,16,384]{3,2,1,0:T(8,128)(2,1)} %get-tuple-element.4.first, bf16[2,4,16,384]{3,2,1,0:T(8,128)(2,1)} %get-tuple-element.5.second), custom_call_target="tpu_custom_call" | custom-call | tf_op jit(solution)/shard_map/pallas_call | solution.py:816

commit v4 on v3

--- a/solution.py
+++ b/solution.py
@@ -10,7 +10,6 @@
 epsilon = 1e-06
 MESH = pl.DeviceIdType.MESH
 bf16, f32 = jnp.bfloat16, jnp.float32
-EXACT = lax.Precision.HIGHEST
 
 
 def normalize(values, gain):
@@ -59,17 +58,24 @@
 
 class Links:
     def __init__(self, send, recv):
-        self.send, self.recv, self.all = send, recv, []
-
-    def copy(self, src, dst, device, sends=True, receives=True):
-        made = Copy(self, len(self.all), src, dst, device, sends, receives)
-        self.all.append(made)
+        self.send, self.recv, self.slots, self.open = send, recv, 0, []
+
+    def copy(self, src, dst, device, sends=True, receives=True, after=None):
+        slot = self.slots if after is None else after.slot
+        self.slots += after is None
+        made = Copy(self, slot, src, dst, device, sends, receives)
+        self.open.append(made)
         return made
 
+    def retire(self, copies):
+        for made in copies:
+            made.drain()
+            self.open.remove(made)
+
     def drain(self):
-        for made in self.all:
+        for made in self.open:
             made.drain()
-        assert len(self.all) == self.send.shape[0], len(self.all)
+        assert self.slots == self.send.shape[0], self.slots
 
 
 class Copy:
@@ -82,7 +88,7 @@
             device_id=device,
             device_id_type=MESH,
         )
-        self.sends, self.receives = sends, receives
+        self.slot, self.sends, self.receives = slot, sends, receives
 
     def start(self):
         when(self.sends, lambda: self.made().start())
@@ -183,7 +189,7 @@
     def block(index):
         return pl.ds(pl.multiple_of(index * W, W), W)
 
-    def gather(source, at, reach):
+    def gather(source, at, reach, after=None):
         arrive = []
         for d in range(1, Z):
             for sign in (1, -1):
@@ -197,7 +203,8 @@
                     src = dst = at(jnp.clip(held, 0, Z - 1))
                 receives = (z >= d) if sign > 0 else (z + d < Z)
                 target = jnp.clip(target, 0, Z - 1)
-                arrive.append((d, z - sign * d, links.copy(src, dst, (s, q, target), sends, receives)))
+                earlier = None if after is None else after[len(arrive)][2]
+                arrive.append((d, z - sign * d, links.copy(src, dst, (s, q, target), sends, receives, earlier)))
         return arrive
 
     def gather_start(arrive, distances):
@@ -219,7 +226,7 @@
                     when(made.receives, functools.partial(use, owner))
 
     class Scatter:
-        def __init__(self, at, landing, hop):
+        def __init__(self, at, landing, hop, after=None):
             self.at, self.landing, self.hop, self.far, self.near = at, landing, hop, {}, {}
             for sign in (1, -1):
                 for D in range(Z - 1, 0, -1):
@@ -231,14 +238,27 @@
                             before = (z >= 1) if sign > 0 else (z < Z - 1)
                             further = (z + D <= Z) if sign > 0 else (z >= D - 1)
                             self.far[sign, D, f] = links.copy(
-                                src, hop.at[int(sign > 0), D - 3, f], (s, q, jnp.clip(z + sign, 0, Z - 1)), sends, both(before, further)
+                                src,
+                                hop.at[int(sign > 0), D - 3, f],
+                                (s, q, jnp.clip(z + sign, 0, Z - 1)),
+                                sends,
+                                both(before, further),
+                                after and after.far[sign, D, f],
                             )
                         else:
                             receives = (z >= D) if sign > 0 else (z + D < Z)
                             slot = 2 * (sign > 0) + D - 1
                             self.near[sign, D, f] = links.copy(
-                                src, landing.at[slot, f], (s, q, jnp.clip(target, 0, Z - 1)), sends, receives
+                                src,
+                                landing.at[slot, f],
+                                (s, q, jnp.clip(target, 0, Z - 1)),
+                                sends,
+                                receives,
+                                after and after.near[sign, D, f],
                             )
+
+        def copies(self):
+            return [*self.far.values(), *self.near.values()]
 
         def start(self, f, distances):
             for D in distances:
@@ -297,9 +317,9 @@
         def _():
             q_next[(sign * d) % Z].start()
 
-    def rows_out(src, dst, device, towards):
+    def rows_out(src, dst, device, towards, after=None):
         sides = (has_high, has_low) if towards > 0 else (has_low, has_high)
-        return links.copy(src, dst, device, *sides)
+        return links.copy(src, dst, device, *sides, after)
 
     q_rows = [
         rows_out(qp.at[own, R], qp.at[own, 0], (s, upper, z), 1),
@@ -313,10 +333,10 @@
         rows_out(xp.at[:, R], xp.at[:, 0], (s, upper, z), 1),
         rows_out(xp.at[:, 1], xp.at[:, R + 1], (s, lower, z), -1),
     ]
-    x_all = gather(act, lambda owner: xp.at[:, body, block(owner)], Z)
+    x_all = gather(act, lambda owner: xp.at[:, body, block(owner)], 2)
     g_out = Scatter(lambda owner, f: gs.at[owner, f], gr, g_hop)
     f_out = [links.copy(fs.at[t], fr.at[t], (nxt, q, z), has_next, has_prev) for t in range(2)]
-    v_all = gather(vall.at[z], lambda owner: vall.at[owner], 2)
+    v_all = gather(vall.at[z], lambda owner: vall.at[owner], 2, x_all)
     sums = [{d: links.copy(st.at[k, 0], st.at[k, d], (s, q, peer(d))) for d in range(1, Z)} for k in range(2)]
     xq_rows = [
         rows_out(xq.at[:, :, R], xq.at[:, :, 0], (s, upper, z), 1),
@@ -327,16 +347,20 @@
     squares_next = links.copy(sq, sh.at[Z], (prv, q, z), has_prev, has_next)
     sums_next = {d: links.copy(st.at[1, 0], sh.at[d], (prv, q, peer(d)), has_prev, has_next) for d in range(Z)}
 
-    def gi_out(frames):
+    def gi_out(frames, after):
         return [
-            rows_out(gi.at[frames, R - 1], gd.at[frames], (s, upper, z), 1),
-            rows_out(gi.at[frames, 0], gu.at[frames], (s, lower, z), -1),
+            rows_out(gi.at[frames, R - 1], gd.at[frames], (s, upper, z), 1, after[0]),
+            rows_out(gi.at[frames, 0], gu.at[frames], (s, lower, z), -1, after[1]),
         ]
 
-    gi_rows, gi_corner = gi_out(own), gi_out(halo)
-    b_out = Scatter(lambda owner, f: yb.at[f, :, block(owner)], rb, b_hop)
-    y_own = {d: links.copy(yf.at[peer(d)], rf.at[z], (s, q, peer(d))) for d in range(1, Z)}
-    y_next = [links.copy(ys.at[t], yr.at[t], (nxt, q, z), has_next, has_prev) for t in range(2)]
+    gi_rows, gi_corner = gi_out(own, q_rows), gi_out(halo, (None, None))
+    b_out = Scatter(lambda owner, f: yb.at[f, :, block(owner)], rb, b_hop, g_out)
+    y_own = {
+        d: links.copy(yf.at[peer(d)], rf.at[z], (s, q, peer(d)), True, True, q_own[1, d]) for d in range(1, Z)
+    }
+    y_next = [
+        links.copy(ys.at[t], yr.at[t], (nxt, q, z), has_next, has_prev, f_out[t]) for t in range(2)
+    ]
 
     lane = lax.broadcasted_iota(jnp.int32, (8, C), 1)
     group = lax.broadcasted_iota(jnp.int32, (8, C), 0)
@@ -352,11 +376,23 @@
     def unpack(packed, m):
         return pad_to(packed[:, m * O : (m + 1) * O], 1, OP)
 
+    segments_three = jnp.concatenate([segments] * 3, axis=1).astype(bf16)
+    segments_down = jnp.concatenate([segments] * 3, axis=0).astype(bf16)
+
+    def thirds(value, axis):
+        high = value.astype(bf16).astype(f32)
+        middle = (value - high).astype(bf16).astype(f32)
+        return jnp.concatenate([high, middle, value - high - middle], axis=axis).astype(bf16)
+
     def segment_sums(value):
-        return lax.dot_general(segments, value, (((1,), (1,)), ((), ())), precision=EXACT, preferred_element_type=f32)
+        return lax.dot_general(
+            segments_three, thirds(value, 1), (((1,), (1,)), ((), ())), preferred_element_type=f32
+        )
 
     def spread(tile):
-        return lax.dot_general(tile, segments, (((0,), (0,)), ((), ())), precision=EXACT, preferred_element_type=f32)
+        return lax.dot_general(
+            thirds(tile, 0), segments_down, (((0,), (0,)), ((), ())), preferred_element_type=f32
+        )
 
     def rhs_forward(w, taps):
         return jnp.concatenate(
@@ -505,7 +541,7 @@
                 w_gap[i, j, l] = jnp.concatenate(
                     [pad_to(w[:, m * O : (m + 1) * O], 1, OP) for m in range(Z)], axis=1
                 ).astype(bf16)
-    gather_start(x_all, range(Z - 1, 0, -1))
+    gather_start(x_all, (2, 1))
     for d in range(1, Z):
         for sign in (1, -1):
             q_pass_on(sign, d)
@@ -530,14 +566,17 @@
     for f in range(F):
         total = early[f] + backward(qp, w_two, f, range(F - f, 3))
         total = shift_sum(total, WW, C)
+        if f == 0:
+            gather_wait(x_all, 2, 2)
         for m in range(Z):
             gs[m, f] = pack(total, m * O).astype(bf16).reshape(R, W, C)
         g_out.start(f, range(Z - 1, 1, -1))
     for f in range(F):
         g_out.start(f, (1,))
 
-    for d in range(1, Z):
-        gather_wait(x_all, d, Z)
+    gather_wait(x_all, 1, 2)
+    for d in range(3, Z):
+        gather_wait(x_all, d, 2)
     for made in x_rows:
         made.start()
     load_one.wait()
@@ -565,11 +604,12 @@
     for d in range(1, Z):
         sums[0][d].start()
 
-    gather_start(v_all, (2,))
     v_next.start()
     grad_two = g_out.total(gs[z].astype(f32)).reshape(rows, C)
     gt[...] = grad_two[: 2 * R * W].astype(bf16).reshape(2, R, W, C)
     g_next.start()
+    links.retire([made for _, _, made in x_all])
+    gather_start(v_all, (2,))
     squares = st[0, 0]
     for d in range(1, Z):
         sums[0][d].wait()
@@ -588,7 +628,7 @@
 
     def activate(owner):
         value = vall[owner].reshape(rows, C).astype(f32)
-        active = silu(value * spread(inverse) * gains[owner][0:1])
+        active = silu(value * inverse_wide * gains[owner][0:1])
         for m in range(Z):
             xq[owner, :, body, m * W : (m + 1) * W] = unpack(active, m).astype(bf16).reshape(F, R, W, OP)
 
@@ -596,6 +636,7 @@
     activate(z)
     gather_wait(v_all, 2, 2, activate)
 
+    links.retire([*(q_own[1, d] for d in range(1, Z)), *f_out, *q_rows, *g_out.copies()])
     means = st[1, 0]
     for d in range(1, Z):
         sums[1][d].wait()
@@ -739,7 +780,7 @@
     taps = kernel_one.shape[:3]
     fold = fold_of(R, O)
     packed = (F, R, W, C)
-    slots = (Z - 1) * (9 + 4 * F) + 2 * Z + 19
+    slots = (Z - 1) * (6 + 2 * F) + 2 * Z + 15
     shapes = [
         kernel_one.shape,
         kernel_two.shape,

time: 51.7 us -> 49.3 us (0.954)
  Pallas kernels: 50.9 us -> 48.5 us
    pallas_call x1, Pallas kernels: 49.3 us -> 46.9 us  [local(): pl.pallas_call(functools.partial(kernel, sizes), out_shape=[jax.ShapeDtyp...]
where the time goes in v4:
time: 49.3 us; the launch traced here: 49.1 us
  Pallas kernels  48.5 us (98%)
  between operations  0.64 us (1%)
    pallas_call x1, Pallas kernels, local(): pl.pallas_call(functools.partial(kernel, sizes), out_shape=[jax.ShapeDtyp...  46.9 us
    pallas_call x1, Pallas kernels, local(): pl.pallas_call(pass_on, out_shape=[jax.ShapeDtypeStruct((F, R, W, C), bf1...  1.62 us

profile of v4, /device:TPU:0, one launch (start us, length us, event | category | flops | bytes accessed | tf_op | source)
XLA Modules:
  0.0 49.1 jit_solution(16547734770163779534)
XLA Ops:
  0.6 46.9 %shard_map.77 = (bf16[2,4,16,384]{3,2,1,0:T(8,128)(2,1)}, bf16[2,4,16,384]{3,2,1,0:T(8,128)(2,1)}) custom-call(bf16[2,4,16,384]{3,2,1,0:T(8,128)(2,1)} %latent_hbm.1, bf16[2,4,16,384]{3,2,1,0:T(8,128)(2,1)} %cotangent_hbm.1, f32[384]{0:T(512)} %gain_one_hbm.1, f32[384]{0:T(512)} %gain_two_hbm.1, bf16[3,3,3,96,384]{4,3,2,1,0:T(8,128)(2,1)} %kernel_one.1, ...), custom_call_target="tpu_custom_call" | custom-call | tf_op jit(solution)/shard_map/pallas_call | solution.py:835
  47.5 1.6 %shard_map.78 = (bf16[2,4,16,384]{3,2,1,0:T(8,128)(2,1)}, bf16[2,4,16,384]{3,2,1,0:T(8,128)(2,1)}) custom-call(bf16[2,4,16,384]{3,2,1,0:T(8,128)(2,1)} %get-tuple-element.4.first, bf16[2,4,16,384]{3,2,1,0:T(8,128)(2,1)} %get-tuple-element.5.second), custom_call_target="tpu_custom_call" | custom-call | tf_op jit(solution)/shard_map/pallas_call | solution.py:857

commit v5 on v4

--- a/solution.py
+++ b/solution.py
@@ -107,12 +107,12 @@
         pl.when(condition)(action)
 
 
-def kernel(sizes, latent_hbm, cotangent_hbm, gain_one_hbm, gain_two_hbm, kernel_one, kernel_two, out_hbm, latent_grad_hbm, *scratch):
+def kernel(sizes, latent_hbm, cotangent_hbm, gain_one_hbm, gain_two_hbm, kernel_one, kernel_two, out, latent_grad, *scratch):
     S, Q, Z = sizes
     (
         w_one, w_two, w_gap, act, xp, qs, qr, qn, qp, gs, gr, fs, fr, vall, st, gains,
         xq, gi, gh, gu, gd, qq, yf, rf, ys, yr, yb, rb, g_hop, b_hop, vh, gt, sq, sh, early,
-        latent, cotangent, gain_one, gain_two, out, latent_grad, send, recv, w_sem, seen,
+        latent, cotangent, gain_one, gain_two, send, recv, w_sem, seen,
     ) = scratch
     F, R, W, C = latent_hbm.shape
     O = kernel_one.shape[3]
@@ -145,10 +145,6 @@
         )
     ]
     load_two, load_one = loads[4:]
-    stores = [
-        pltpu.make_async_copy(out, out_hbm, w_sem.at[6]),
-        pltpu.make_async_copy(latent_grad, latent_grad_hbm, w_sem.at[7]),
-    ]
     for load in loads[:4]:
         load.start()
 
@@ -337,15 +333,23 @@
     g_out = Scatter(lambda owner, f: gs.at[owner, f], gr, g_hop)
     f_out = [links.copy(fs.at[t], fr.at[t], (nxt, q, z), has_next, has_prev) for t in range(2)]
     v_all = gather(vall.at[z], lambda owner: vall.at[owner], 2, x_all)
-    sums = [{d: links.copy(st.at[k, 0], st.at[k, d], (s, q, peer(d))) for d in range(1, Z)} for k in range(2)]
+    sums = [
+        {
+            d: links.copy(st.at[k, 0], st.at[k, d], (s, q, peer(d)), True, True, q_own[-1, d] if k else None)
+            for d in range(1, Z)
+        }
+        for k in range(2)
+    ]
     xq_rows = [
         rows_out(xq.at[:, :, R], xq.at[:, :, 0], (s, upper, z), 1),
         rows_out(xq.at[:, :, 1], xq.at[:, :, R + 1], (s, lower, z), -1),
     ]
-    v_next = links.copy(vall.at[z, two], vh, (prv, q, z), has_prev, has_next)
-    g_next = links.copy(gt, gh, (prv, q, z), has_prev, has_next)
+    v_next = links.copy(vall.at[z, two], vh, (prv, q, z), has_prev, has_next, q_corner[0])
+    g_next = links.copy(gt, gh, (prv, q, z), has_prev, has_next, q_corner[1])
     squares_next = links.copy(sq, sh.at[Z], (prv, q, z), has_prev, has_next)
-    sums_next = {d: links.copy(st.at[1, 0], sh.at[d], (prv, q, peer(d)), has_prev, has_next) for d in range(Z)}
+    sums_next = {
+        d: links.copy(st.at[1, 0], sh.at[d], (prv, q, peer(d)), has_prev, has_next, q_next[d]) for d in range(Z)
+    }
 
     def gi_out(frames, after):
         return [
@@ -604,6 +608,7 @@
     for d in range(1, Z):
         sums[0][d].start()
 
+    links.retire([*q_own.values(), *q_next.values(), *q_corner])
     v_next.start()
     grad_two = g_out.total(gs[z].astype(f32)).reshape(rows, C)
     gt[...] = grad_two[: 2 * R * W].astype(bf16).reshape(2, R, W, C)
@@ -636,7 +641,7 @@
     activate(z)
     gather_wait(v_all, 2, 2, activate)
 
-    links.retire([*(q_own[1, d] for d in range(1, Z)), *f_out, *q_rows, *g_out.copies()])
+    links.retire([*f_out, *q_rows, *g_out.copies()])
     means = st[1, 0]
     for d in range(1, Z):
         sums[1][d].wait()
@@ -664,6 +669,7 @@
             def _():
                 place(ref[frames], frames, row, count * W)
 
+    gather_wait(v_all, 1, 2, activate)
     for made in (v_next, g_next, squares_next):
         made.wait()
     for d in range(Z):
@@ -690,7 +696,6 @@
 
     for made in gi_corner:
         made.start()
-    gather_wait(v_all, 1, 2, activate)
     for d in range(3, Z):
         gather_wait(v_all, d, 2, activate)
     for made in xq_rows:
@@ -706,9 +711,10 @@
     for f in range(F):
         total = early[f] + backward(qq, w_one, f, range(F - f, 3))
         yb[f] = shift_sum(total, WW, C).astype(bf16).reshape(R, WW, C)
-        b_out.start(f, range(Z - 1, 1, -1))
-    for f in range(F):
-        b_out.start(f, (1,))
+        b_out.start(f, range(Z - 1, 2, -1))
+    for d in (2, 1):
+        for f in range(F):
+            b_out.start(f, (d,))
 
     def lhs_two(f):
         return jnp.concatenate(
@@ -738,25 +744,18 @@
         y_own[d].start()
     rf[z] = yf[z]
 
+    source = latent[...].reshape(rows, C).astype(f32)
+    normed_one, inverse_one = normalize(source, g_one)
+    slope_one = silu_slope(normed_one)
+    upstream = cotangent[...].reshape(rows, C).astype(f32)
+    grad_one = b_out.total(yb[:, :, block(z)].astype(f32)).reshape(rows, C)
+    grad = norm_backward(source, inverse_one, g_one, grad_one * slope_one)
+    latent_grad[...] = (upstream + grad).astype(bf16).reshape(F, R, W, C)
     for d in range(1, Z):
         y_own[d].wait()
-    chunks = []
-    for m in range(Z):
-        chunks.append(unfold_rows(rf[m], O).reshape(rows, O))
-    branch = jnp.concatenate(chunks, axis=1)
-    source = latent[...].reshape(rows, C).astype(f32)
+    branch = jnp.concatenate([unfold_rows(rf[m], O).reshape(rows, O) for m in range(Z)], axis=1)
     out[...] = (source + branch).astype(bf16).reshape(F, R, W, C)
-    stores[0].start()
-
-    grad_one = b_out.total(yb[:, :, block(z)].astype(f32)).reshape(rows, C)
-    normed_one, inverse_one = normalize(source, g_one)
-    grad = norm_backward(source, inverse_one, g_one, grad_one * silu_slope(normed_one))
-    upstream = cotangent[...].reshape(rows, C).astype(f32)
-    latent_grad[...] = (upstream + grad).astype(bf16).reshape(F, R, W, C)
-    stores[1].start()
     links.drain()
-    for store in stores:
-        store.wait()
 
 
 def hand_over(first, second, first_out, second_out, sem):
@@ -780,7 +779,7 @@
     taps = kernel_one.shape[:3]
     fold = fold_of(R, O)
     packed = (F, R, W, C)
-    slots = (Z - 1) * (6 + 2 * F) + 2 * Z + 15
+    slots = (Z - 1) * (5 + 2 * F) + Z + 13
     shapes = [
         kernel_one.shape,
         kernel_two.shape,
@@ -821,8 +820,6 @@
         packed,
         None,
         None,
-        packed,
-        packed,
     ]
     scratch = [pltpu.VMEM(shape, bf16) if shape else None for shape in shapes]
     scratch[14] = pltpu.VMEM((2, Z, 8, rows), f32)
@@ -836,30 +833,26 @@
         functools.partial(kernel, sizes),
         out_shape=[jax.ShapeDtypeStruct((F, R, W, C), bf16)] * 2,
         in_specs=[hbm] * 6,
-        out_specs=[hbm] * 2,
+        out_specs=[pl.BlockSpec(memory_space=pltpu.VMEM)] * 2,
         scratch_shapes=[
             *scratch,
             pltpu.SemaphoreType.DMA((slots,)),
             pltpu.SemaphoreType.DMA((slots,)),
-            pltpu.SemaphoreType.DMA((8,)),
+            pltpu.SemaphoreType.DMA((6,)),
             pltpu.SemaphoreType.REGULAR((2, max(Z - 2, 1))),
         ],
         compiler_params=pltpu.CompilerParams(
-            collective_id=0, has_side_effects=True, vmem_limit_bytes=60 * 1024 * 1024
+            collective_id=0, has_side_effects=True, vmem_limit_bytes=28 * 1024 * 1024
         ),
-    )(latent, cotangent, gain_one, gain_two, kernel_one, kernel_two)
+    )(*[pltpu.with_memory_space_constraint(a, pltpu.HBM) for a in (latent, cotangent, gain_one, gain_two, kernel_one, kernel_two)])
     vmem = pl.BlockSpec(memory_space=pltpu.VMEM)
-
-    def pass_on(first, second, first_out, second_out):
-        first_out[...] = first[...]
-        second_out[...] = second[...]
-
     return pl.pallas_call(
-        pass_on,
+        hand_over,
         out_shape=[jax.ShapeDtypeStruct((F, R, W, C), bf16)] * 2,
         in_specs=[vmem] * 2,
-        out_specs=[vmem] * 2,
-    )(*results)
+        out_specs=[hbm] * 2,
+        scratch_shapes=[pltpu.SemaphoreType.DMA((2,))],
+    )(*[pltpu.with_memory_space_constraint(a, pltpu.VMEM) for a in results])
 
 def solution(mesh):
     sizes = (mesh.shape["section"], mesh.shape["seq"], mesh.shape["exp"])

time: 49.3 us -> 47.4 us (0.961)
  Pallas kernels: 48.5 us -> 46.6 us
    pallas_call x1, Pallas kernels: 46.9 us -> 45.9 us  [local(): pl.pallas_call(functools.partial(kernel, sizes), out_shape=[jax.ShapeDtyp...]
    pallas_call x1, Pallas kernels: 1.62 us -> 0.69 us  [local(): pl.pallas_call(hand_over, out_shape=[jax.ShapeDtypeStruct((F, R, W, C), b...]
where the time goes in v5:
time: 47.4 us; the launch traced here: 47.3 us
  Pallas kernels  46.6 us (98%)
  between operations  0.64 us (1%)
    pallas_call x1, Pallas kernels, local(): pl.pallas_call(functools.partial(kernel, sizes), out_shape=[jax.ShapeDtyp...  45.9 us

profile of v5, /device:TPU:0, one launch (start us, length us, event | category | flops | bytes accessed | tf_op | source)
XLA Modules:
  0.0 47.3 jit_solution(8334523925547352443)
XLA Ops:
  0.6 45.9 %shard_map.77 = (bf16[2,4,16,384]{3,2,1,0:T(8,128)(2,1)S(1)}, bf16[2,4,16,384]{3,2,1,0:T(8,128)(2,1)S(1)}) custom-call(bf16[2,4,16,384]{3,2,1,0:T(8,128)(2,1)} %latent_hbm.1, bf16[2,4,16,384]{3,2,1,0:T(8,128)(2,1)} %cotangent_hbm.1, f32[384]{0:T(512)} %gain_one_hbm.1, f32[384]{0:T(512)} %gain_two_hbm.1, bf16[3,3,3,96,384]{4,3,2,1,0:T(8,128)(2,1)} %kernel_one.1, ...), custom_call_target="tpu_custom_call" | custom-call | tf_op jit(solution)/shard_map/pallas_call | solution.py:832
  46.6 0.7 %shard_map.78 = (bf16[2,4,16,384]{3,2,1,0:T(8,128)(2,1)}, bf16[2,4,16,384]{3,2,1,0:T(8,128)(2,1)}) custom-call(bf16[2,4,16,384]{3,2,1,0:T(8,128)(2,1)S(1)} %get-tuple-element.4.first, bf16[2,4,16,384]{3,2,1,0:T(8,128)(2,1)S(1)} %get-tuple-element.5.second), custom_call_target="tpu_custom_call" | custom-call | tf_op jit(solution)/shard_map/pallas_call | solution.py:849

commit v6 on v5

--- a/solution.py
+++ b/solution.py
@@ -639,7 +639,6 @@
 
     gather_start(v_all, (1,))
     activate(z)
-    gather_wait(v_all, 2, 2, activate)
 
     links.retire([*f_out, *q_rows, *g_out.copies()])
     means = st[1, 0]
@@ -661,6 +660,7 @@
             )
 
     place(gi[own], own, body, rows)
+    gather_wait(v_all, 2, 2, activate)
 
     def place_rows(frames, count, among):
         for side, ref, row in ((has_low, gd, 0), (has_high, gu, R + 1)):
@@ -669,7 +669,6 @@
             def _():
                 place(ref[frames], frames, row, count * W)
 
-    gather_wait(v_all, 1, 2, activate)
     for made in (v_next, g_next, squares_next):
         made.wait()
     for d in range(Z):
@@ -696,10 +695,6 @@
 
     for made in gi_corner:
         made.start()
-    for d in range(3, Z):
-        gather_wait(v_all, d, 2, activate)
-    for made in xq_rows:
-        made.start()
     for made in gi_rows:
         made.wait()
     place_rows(own, F, None)
@@ -712,6 +707,12 @@
         total = early[f] + backward(qq, w_one, f, range(F - f, 3))
         yb[f] = shift_sum(total, WW, C).astype(bf16).reshape(R, WW, C)
         b_out.start(f, range(Z - 1, 2, -1))
+        if f == 0:
+            gather_wait(v_all, 1, 2, activate)
+            for d in range(3, Z):
+                gather_wait(v_all, d, 2, activate)
+            for made in xq_rows:
+                made.start()
     for d in (2, 1):
         for f in range(F):
             b_out.start(f, (d,))

time: 47.4 us -> 47.4 us (level)
  no operation moved by 1% of the time
where the time goes in v6:
time: 47.4 us; the launch traced here: 47.2 us
  Pallas kernels  46.6 us (98%)
  between operations  0.64 us (1%)
    pallas_call x1, Pallas kernels, local(): pl.pallas_call(functools.partial(kernel, sizes), out_shape=[jax.ShapeDtyp...  45.9 us

profile of v6, /device:TPU:0, one launch (start us, length us, event | category | flops | bytes accessed | tf_op | source)
XLA Modules:
  0.0 47.2 jit_solution(14547704967964322067)
XLA Ops:
  0.6 45.9 %shard_map.77 = (bf16[2,4,16,384]{3,2,1,0:T(8,128)(2,1)S(1)}, bf16[2,4,16,384]{3,2,1,0:T(8,128)(2,1)S(1)}) custom-call(bf16[2,4,16,384]{3,2,1,0:T(8,128)(2,1)} %latent_hbm.1, bf16[2,4,16,384]{3,2,1,0:T(8,128)(2,1)} %cotangent_hbm.1, f32[384]{0:T(512)} %gain_one_hbm.1, f32[384]{0:T(512)} %gain_two_hbm.1, bf16[3,3,3,96,384]{4,3,2,1,0:T(8,128)(2,1)} %kernel_one.1, ...), custom_call_target="tpu_custom_call" | custom-call | tf_op jit(solution)/shard_map/pallas_call | solution.py:833
  46.5 0.7 %shard_map.78 = (bf16[2,4,16,384]{3,2,1,0:T(8,128)(2,1)}, bf16[2,4,16,384]{3,2,1,0:T(8,128)(2,1)}) custom-call(bf16[2,4,16,384]{3,2,1,0:T(8,128)(2,1)S(1)} %get-tuple-element.4.first, bf16[2,4,16,384]{3,2,1,0:T(8,128)(2,1)S(1)} %get-tuple-element.5.second), custom_call_target="tpu_custom_call" | custom-call | tf_op jit(solution)/shard_map/pallas_call | solution.py:850

commit v7 on v6

--- a/solution.py
+++ b/solution.py
@@ -428,9 +428,7 @@
             return functools.reduce(lambda a, b: a + b, parts[t])
 
         def ahead(t):
-            if not parts:
-                for f in range(F - 1, max(F - 3, -1), -1):
-                    run(f, (0, 1))
+            run(t - 2, (0, 1))
             return finish(t)
 
         def rest(t):

time: 47.4 us -> 47.4 us (level)
  no operation moved by 1% of the time
where the time goes in v7:
time: 47.4 us; the launch traced here: 47.3 us
  Pallas kernels  46.6 us (98%)
  between operations  0.64 us (1%)
    pallas_call x1, Pallas kernels, local(): pl.pallas_call(functools.partial(kernel, sizes), out_shape=[jax.ShapeDtyp...  45.9 us

profile of v7, /device:TPU:0, one launch (start us, length us, event | category | flops | bytes accessed | tf_op | source)
XLA Modules:
  0.0 47.3 jit_solution(3043885539460629294)
XLA Ops:
  0.6 45.9 %shard_map.77 = (bf16[2,4,16,384]{3,2,1,0:T(8,128)(2,1)S(1)}, bf16[2,4,16,384]{3,2,1,0:T(8,128)(2,1)S(1)}) custom-call(bf16[2,4,16,384]{3,2,1,0:T(8,128)(2,1)} %latent_hbm.1, bf16[2,4,16,384]{3,2,1,0:T(8,128)(2,1)} %cotangent_hbm.1, f32[384]{0:T(512)} %gain_one_hbm.1, f32[384]{0:T(512)} %gain_two_hbm.1, bf16[3,3,3,96,384]{4,3,2,1,0:T(8,128)(2,1)} %kernel_one.1, ...), custom_call_target="tpu_custom_call" | custom-call | tf_op jit(solution)/shard_map/pallas_call | solution.py:831
  46.6 0.7 %shard_map.78 = (bf16[2,4,16,384]{3,2,1,0:T(8,128)(2,1)}, bf16[2,4,16,384]{3,2,1,0:T(8,128)(2,1)}) custom-call(bf16[2,4,16,384]{3,2,1,0:T(8,128)(2,1)S(1)} %get-tuple-element.4.first, bf16[2,4,16,384]{3,2,1,0:T(8,128)(2,1)S(1)} %get-tuple-element.5.second), custom_call_target="tpu_custom_call" | custom-call | tf_op jit(solution)/shard_map/pallas_call | solution.py:848
